TPU v7x, 32 devices: a whole 2x2x4 slice. The times are simulated.
32 devices in a mesh: row: 2 (over core), col: 16 (over z, y, x).
Axes of the slice: x: 2, y: 2, z: 4, core: 2. Of those that a mesh axis runs over, the one named last changes fastest.
Arguments:
- object_in: float32 [2, 2, 512, 4096], P(None, None, 'row', 'col'), may hold values from -4 to 4
- probe_in: float32 [2, 256, 256], replicated, may hold values from -5 to 5
- positions: int32 [2, 16, 2, 2], P('row', 'col'), may hold values from -32 to 32
- intensity: float32 [2, 16, 2, 256, 256], P('row', 'col'), may hold values from 0.1 to 8.2
Outputs:
- object_out: float32 [2, 2, 512, 4096], P(None, None, 'row', 'col')
- probe_out: float32 [2, 256, 256], replicated
Inputs may be any that keep to these rules, and one draw needn't show every extreme that they name: positions[r, c, p] = (dy, dx) places the probe of position p on object rows r * 256 + dy to r * 256 + dy + 255 and columns c * 256 + dx to c * 256 + dx + 255.
All inputs are finite; a program needn't handle non-finite values.
Results may differ from a plain program's by a relative error of at most 0.0003.
Values sent between devices are 32-bit elements; how exact they have to be, the bound alone decides.
No kernel may reach another device: no remote copies, remote signals or barrier semaphores. Data moves between devices by JAX's collectives and lax.ppermute only.
A program may use at most 64 MiB of HBM per device.

v0:
```python
import math

import jax
import jax.numpy as jnp
from jax import lax
from jax.sharding import PartitionSpec as P

RIM = 32


def passed_along(value, axis, steps):
    count = lax.axis_size(axis)
    initial, last = (max(0, -steps), min(count, count - steps))
    return lax.ppermute(value, axis, [(source, source + steps) for source in range(initial, last)])


def extended(cells, sides, width):
    for axis, dim in sides:
        count = lax.axis_size(axis)
        ends = count - 1
        head = lax.slice_in_dim(cells, 0, width, axis=dim)
        tail = lax.slice_in_dim(cells, cells.shape[dim] - width, cells.shape[dim], axis=dim)
        cells = jnp.concatenate(
            [
                lax.ppermute(tail, axis, [(i, (i + 1) % count) for i in range(ends)]),
                cells,
                lax.ppermute(head, axis, [((i + 1) % count, i) for i in range(ends)]),
            ],
            axis=dim,
        )
    return cells


def tables(extent):
    line_idx = jnp.arange(extent, dtype=jnp.int32)
    turn_count = line_idx[:, None] * line_idx[None, :] % extent
    angles = turn_count.astype(jnp.float32) * (2.0 * math.pi / extent)
    factor = 1.0 / math.sqrt(extent)
    cosine = jnp.cos(angles) * factor
    sine_tab = jnp.sin(angles) * factor
    frequency = ((line_idx + extent // 2) % extent - extent // 2).astype(jnp.float32)
    phases = (
        -math.pi * 8.0 / (extent * extent) * (frequency[:, None] ** 2 + frequency[None, :] ** 2)
    )
    return (cosine, sine_tab, jnp.cos(phases), jnp.sin(phases))


def matrices(cosine, sine_tab, orient):
    return (cosine, sine_tab, float(orient))


def transform(real_part, imag_part, tables_pair):
    cosine, sine_tab, orient = tables_pair
    high = lax.Precision.HIGHEST
    rc = jnp.einsum("byx,xk->byk", real_part, cosine, precision=high)
    rs = jnp.einsum("byx,xk->byk", real_part, sine_tab, precision=high)
    ic = jnp.einsum("byx,xk->byk", imag_part, cosine, precision=high)
    isn = jnp.einsum("byx,xk->byk", imag_part, sine_tab, precision=high)
    mid_re = rc + orient * isn
    mid_im = ic - orient * rs
    out_re = jnp.einsum("ky,byx->bkx", cosine, mid_re, precision=high) + orient * jnp.einsum(
        "ky,byx->bkx", sine_tab, mid_im, precision=high
    )
    out_im = jnp.einsum("ky,byx->bkx", cosine, mid_im, precision=high) - orient * jnp.einsum(
        "ky,byx->bkx", sine_tab, mid_re, precision=high
    )
    return (out_re, out_im)


def times_plain(first_re, first_im, second_re, second_im):
    return (
        first_re * second_re - first_im * second_im,
        first_re * second_im + first_im * second_re,
    )


def times_conj(first_re, first_im, second_re, second_im):
    return (
        first_re * second_re + first_im * second_im,
        first_re * second_im - first_im * second_re,
    )


def tile_gradient(window, probe, offsets, measured, constants):
    cosine, sine_tab, kern_re, kern_im = constants
    forward = matrices(cosine, sine_tab, 1)
    backward = matrices(cosine, sine_tab, -1)
    extent = probe.shape[-1]
    zero_idx = jnp.zeros((), jnp.int32)

    def cut_patch(offset):
        return lax.dynamic_slice(
            window, (zero_idx, zero_idx, offset[0] + RIM, offset[1] + RIM), (2, 2, extent, extent)
        )

    patches = jax.vmap(cut_patch)(offsets)
    first_re, first_im = (patches[:, 0, 0], patches[:, 0, 1])
    second_re, second_im = (patches[:, 1, 0], patches[:, 1, 1])
    probe_re, probe_im = (probe[0], probe[1])
    wave_re, wave_im = times_plain(probe_re, probe_im, first_re, first_im)
    spec_re, spec_im = transform(wave_re, wave_im, forward)
    spec_re, spec_im = times_plain(kern_re, kern_im, spec_re, spec_im)
    prop_re, prop_im = transform(spec_re, spec_im, backward)
    exit_re, exit_im = times_plain(prop_re, prop_im, second_re, second_im)
    far_re, far_im = transform(exit_re, exit_im, forward)
    excess = 2.0 * (far_re * far_re + far_im * far_im - measured)
    back_re, back_im = transform(excess * far_re, excess * far_im, backward)
    grad2_re, grad2_im = times_conj(prop_re, prop_im, back_re, back_im)
    lift_re, lift_im = times_conj(second_re, second_im, back_re, back_im)
    lift_re, lift_im = transform(lift_re, lift_im, forward)
    lift_re, lift_im = times_conj(kern_re, kern_im, lift_re, lift_im)
    enter_re, enter_im = transform(lift_re, lift_im, backward)
    grad1_re, grad1_im = times_conj(probe_re, probe_im, enter_re, enter_im)
    probe_re_g, probe_im_g = times_conj(first_re, first_im, enter_re, enter_im)
    probe_grad = jnp.stack([jnp.sum(probe_re_g, 0), jnp.sum(probe_im_g, 0)], 0)
    pieces = jnp.stack([jnp.stack([grad1_re, grad1_im], 1), jnp.stack([grad2_re, grad2_im], 1)], 1)
    gradient = jnp.zeros(window.shape, jnp.float32)
    for position in range(offsets.shape[0]):
        start_at = (zero_idx, zero_idx, offsets[position, 0] + RIM, offsets[position, 1] + RIM)
        current = lax.dynamic_slice(gradient, start_at, pieces.shape[1:])
        gradient = lax.dynamic_update_slice(gradient, current + pieces[position], start_at)
    return (gradient, probe_grad)


def turned(block):
    return jnp.swapaxes(block, 2, 3)


def rows_then_cols(gradient):
    inner_px = gradient.shape[-1] - 2 * RIM
    upper_end = RIM + inner_px
    from_below = passed_along(gradient[:, :, :RIM, :], "row", -1)
    from_above = passed_along(gradient[:, :, upper_end:, :], "row", 1)
    middle = gradient[:, :, RIM:upper_end, :]
    middle = middle.at[:, :, inner_px - RIM :, :].add(from_below)
    middle = middle.at[:, :, :RIM, :].add(from_above)
    from_right = turned(passed_along(turned(middle[..., :RIM]), "col", -1))
    from_left = turned(passed_along(turned(middle[..., upper_end:]), "col", 1))
    interior = middle[..., RIM:upper_end]
    interior = interior.at[..., inner_px - RIM :].add(from_right)
    interior = interior.at[..., :RIM].add(from_left)
    return interior


def local(object_in, probe_in, positions, intensity):
    extent = probe_in.shape[-1]
    constants = tables(extent)
    offsets = positions.reshape(-1, 2)
    measured = intensity.reshape(-1, extent, extent)
    tile_total = lax.axis_size("row") * lax.axis_size("col")
    probe_rate = 2.0 / tile_total
    current = object_in
    window = extended(current, (("row", 2), ("col", 3)), RIM)
    gradient, probe_grad = tile_gradient(window, probe_in, offsets, measured, constants)
    probe_total = lax.psum(probe_grad, ("row", "col"))
    probe_next = probe_in - probe_rate * probe_total
    descent = rows_then_cols(gradient)
    local_peak = jnp.max(descent[:, 0] ** 2 + descent[:, 1] ** 2)
    largest = lax.pmax(local_peak, ("row", "col"))
    current = current - 0.3 * descent / (jnp.sqrt(largest) + 1e-06)
    return (current, probe_next)


def solution(mesh):
    placed = (
        P(None, None, "row", "col"),
        P(),
        P("row", "col", None, None),
        P("row", "col", None, None, None),
    )
    return jax.shard_map(
        local,
        mesh=mesh,
        in_specs=placed,
        out_specs=(P(None, None, "row", "col"), P()),
        check_vma=False,
    )
```

profile of v0, /device:TPU:0, one launch (start us, length us, event | category | flops | bytes accessed | tf_op | source)
XLA Modules:
  0.0 372.6 jit_solution(18278796465916017940)
XLA Ops:
  10.1 2.4 collective-permute-start
  22.2 2.0 copy.98
  24.5 4.2 %collective-permute-start.2 = (f32[2,2,320,32]{2,3,1,0:T(8,128)S(1)}, f32[2,2,320,32]{2,3,1,0:T(8,128)S(1)}, u32[]{:S(2)}, u32[]{:S(2)}) collective-permute-start(f32[2,2,320,32]{2,3,1,0:T(8,128)S(1)} %get-tuple-element.84), channel_id=1, source_target_pairs={{0,1},{1,2},{2,3},{3,4},{4,5},{5,6},{6,7},{7,8},{8,9},{9,10},{10,1... | collective-permute-start | bytes 491528 | tf_op jit(solution)/shard_map/ppermute | solution.py:25
  30.1 3.7 collective-permute-done.2
  33.8 6.2 %collective-permute-done.3 = f32[2,2,320,32]{2,3,1,0:T(8,128)S(1)} collective-permute-done((f32[2,2,320,32]{2,3,1,0:T(8,128)S(1)}, f32[2,2,320,32]{2,3,1,0:T(8,128)S(1)}, u32[]{:S(2)}, u32[]{:S(2)}) %collective-permute-start.3) | collective-permute-done | bytes 163872 | tf_op jit(solution)/shard_map/ppermute | solution.py:27
  41.8 11.3 %while.5 = (s32[]{:T(128)}, f32[2,2,320,320]{2,3,1,0:T(8,128)S(1)}, s32[2,4]{1,0:T(2,128)S(1)}, f32[2,2,2,256,256]{3,4,0,2,1:T(8,128)}, s32[]{:T(128)}) while((s32[]{:T(128)}, f32[2,2,320,320]{2,3,1,0:T(8,128)S(1)}, s32[2,4]{1,0:T(2,128)S(1)}, f32[2,2,2,256,256]{3,4,0,2,1:T(8,128)}, s32[]{:T(128)}) %tuple.62), condition=%wide.while_cond.4, body=%wide.while_body.4.sunk | while | flops 2 | bytes 21496496 | solution.py:92
  53.1 3.4 fusion.112
  56.5 3.2 fusion.116
  59.8 1.9 convolution_subtract_fusion.5
  63.5 1.9 convolution_add_fusion.5
  67.2 2.3 fusion.22
  71.4 1.9 fusion.108
  73.3 1.9 fusion.104
  75.1 1.9 fusion.21
  78.8 2.1 fusion.20
  84.5 1.9 fusion.32
  90.1 2.0 convolution_add_fusion.3
  94.0 1.8 convolution_subtract_fusion.3
  95.9 1.8 fusion.94
  97.7 1.8 fusion.15
  99.5 1.8 fusion.14
  101.4 1.9 fusion.92
  103.3 2.3 fusion.88
  105.7 1.9 fusion.13
  107.6 1.9 fusion.12
  115.0 2.2 add_bitcast_fusion
  119.0 1.8 fusion.84
  120.9 1.9 convolution_subtract_fusion.1
  124.6 1.8 convolution_add_fusion.1
  126.4 2.1 fusion.82
  128.5 1.8 fusion.6
  130.3 1.8 fusion.7
  132.2 1.9 fusion.76
  134.1 1.9 fusion.72
  136.0 1.9 fusion.5
  137.9 2.3 fusion.4
  145.6 2.8 fusion.38
  150.0 14.2 %dynamic_update_slice.6 = f32[2,2,320,320]{2,3,1,0:T(8,128)S(1)} dynamic-update-slice(f32[2,2,320,320]{2,3,1,0:T(8,128)S(1)} %broadcast_in_dim.2, f32[2,2,256,256]{2,3,1,0:T(8,128)} %fusion.25, s32[]{:T(128)} %constant.162.clone.1, s32[]{:T(128)} %constant.162.clone.1, s32[]{:T(128)S(6)} %select_n.155, s32[]{:T(128)S(6)} %select_n.156) | dynamic-update-slice | bytes 2097156 | tf_op jit(solution)/shard_map/dynamic_update_slice | solution.py:121
  164.2 2.4 fusion.27
  166.6 13.5 %dynamic_update_slice.7 = f32[2,2,320,320]{2,3,1,0:T(8,128)S(1)} dynamic-update-slice(f32[2,2,320,320]{2,3,1,0:T(8,128)S(1)} %dynamic_update_slice.6, f32[2,2,256,256]{2,3,1,0:T(8,128)} %fusion.27, s32[]{:T(128)} %constant.162.clone.1, s32[]{:T(128)} %constant.162.clone.1, s32[]{:T(128)S(6)} %select_n.157, s32[]{:T(128)S(6)} %select_n.158) | dynamic-update-slice | bytes 2097156 | tf_op jit(solution)/shard_map/dynamic_update_slice | solution.py:121
  182.0 2.0 copy.129
  187.3 4.4 %collective-permute-start.5 = (f32[2,2,32,320]{3,2,1,0:T(8,128)}, f32[2,2,32,320]{3,2,1,0:T(8,128)}, u32[]{:S(2)}, u32[]{:S(2)}) collective-permute-start(f32[2,2,32,320]{3,2,1,0:T(8,128)} %copy.126), channel_id=1, source_target_pairs={{0,16},{1,17},{2,18},{3,19},{4,20},{5,21},{6,22},{7,23},{8,24},{9,... | collective-permute-start | bytes 491528 | tf_op jit(solution)/shard_map/ppermute | solution.py:14
  193.0 3.8 %scatter-add.14 = f32[2,2,256,320]{2,3,1,0:T(8,128)} dynamic-update-slice(f32[2,2,256,320]{2,3,1,0:T(8,128)} %slice.249, f32[2,2,32,320]{2,3,1,0:T(8,128)S(1)} %slice_add_fusion.1, s32[]{:T(128)} %constant.162.clone.1, s32[]{:T(128)} %constant.162.clone.1, s32[]{:T(128)} %constant.175.clone.1, s32[]{:T(128)} %constant.162.clone.1) | dynamic-update-slice | bytes 327684 | tf_op jit(solution)/shard_map/scatter-add | solution.py:135
  199.1 3.6 scatter-add.15
  207.0 4.7 %collective-permute-start.7 = (f32[2,2,32,256]{3,2,1,0:T(8,128)S(1)}, f32[2,2,32,256]{3,2,1,0:T(8,128)S(1)}, u32[]{:S(2)}, u32[]{:S(2)}) collective-permute-start(f32[2,2,32,256]{3,2,1,0:T(8,128)S(1)} %get-tuple-element.90), channel_id=1, source_target_pairs={{0,1},{1,2},{2,3},{3,4},{4,5},{5,6},{6,7},{7,8},{8,9},{9,10},{10,1... | collective-permute-start | bytes 393224 | tf_op jit(solution)/shard_map/ppermute | solution.py:14
  211.7 106.0 %all-reduce.2.cloned.1.call-done = f32[2,256,256]{1,2,0:T(8,128)} async-done(((f32[2,256,256]{1,2,0:T(8,128)}), f32[2,256,256]{1,2,0:T(8,128)}) %all-reduce.2.cloned.1.call-update) | async-done | bytes 524304 | tf_op jit(solution)/shard_map/psum | solution.py:155
  321.6 39.5 %pmax.7 = f32[]{:T(128)} all-reduce(f32[]{:T(128)} %fusion.29), channel_id=1, replica_groups=mesh['row'=2,'col'=16] {'row','col'}, use_global_device_ids=true, to_apply=%region_1.2 | all-reduce | flops 1 | bytes 8 | tf_op jit(solution)/shard_map/pmax | solution.py:159
  363.0 2.5 copy.130
  (113 shorter events, 72.5 us)
Async XLA Ops:
  7.2 6.7 %copy-start.15 = (s32[1,1,2,2]{3,2,1,0:T(2,128)S(1)}, s32[1,1,2,2]{3,2,1,0:T(2,128)}, u32[]{:S(2)}) copy-start(s32[1,1,2,2]{3,2,1,0:T(2,128)} %param.14) | copy-start | bytes 52
  7.2 12.2 %copy-start.12 = (f32[2,256,256]{2,1,0:T(8,128)S(1)}, f32[2,256,256]{2,1,0:T(8,128)}, u32[]{:S(2)}) copy-start(f32[2,256,256]{2,1,0:T(8,128)} %param.13) | copy-start | bytes 1572868
  7.2 310.5 %all-reduce.2.cloned.1.call-start = ((), (), s32[]{:S(2)}) async-start(), calls=%async_computation | async-start | bytes 1048576 | tf_op jit(solution)/shard_map/psum | solution.py:155
  8.8 31.1 %copy-start.2 = (f32[2,2,256,256]{2,3,1,0:T(8,128)}, f32[2,2,256,256]{2,3,1,0:T(8,128)S(1)}, u32[]{:S(2)}) copy-start(f32[2,2,256,256]{2,3,1,0:T(8,128)S(1)} %copy.128) | copy-start | bytes 3145732
  10.1 14.2 %collective-permute-start = (f32[2,2,32,256]{2,3,1,0:T(8,128)}, f32[2,2,32,256]{2,3,1,0:T(8,128)S(1)}, u32[]{:S(2)}, u32[]{:S(2)}) collective-permute-start(f32[2,2,32,256]{2,3,1,0:T(8,128)} %get-tuple-element.96), channel_id=1, source_target_pairs={{0,16},{1,17},{2,18},{3,19},{4,20},{5,21},{6,22},{7,23},{8,24},{9,... | collective-permute-start | bytes 393224 | tf_op jit(solution)/shard_map/ppermute | solution.py:25
  12.5 11.7 %collective-permute-start.1 = (f32[2,2,32,256]{2,3,1,0:T(8,128)}, f32[2,2,32,256]{2,3,1,0:T(8,128)S(1)}, u32[]{:S(2)}, u32[]{:S(2)}) collective-permute-start(f32[2,2,32,256]{2,3,1,0:T(8,128)} %get-tuple-element.97), channel_id=1, source_target_pairs={{16,0},{17,1},{18,2},{19,3},{20,4},{21,5},{22,6},{23,7},{24,8},{25... | collective-permute-start | bytes 393224 | tf_op jit(solution)/shard_map/ppermute | solution.py:27
  24.3 9.5 %copy-start.9 = (f32[2,2,32,256]{2,3,1,0:T(8,128)}, f32[2,2,32,256]{2,3,1,0:T(8,128)S(1)}, u32[]{:S(2)}) copy-start(f32[2,2,32,256]{2,3,1,0:T(8,128)S(1)} %collective-permute-done) | copy-start | bytes 393220
  24.3 9.5 %copy-start.10 = (f32[2,2,32,256]{2,3,1,0:T(8,128)}, f32[2,2,32,256]{2,3,1,0:T(8,128)S(1)}, u32[]{:S(2)}) copy-start(f32[2,2,32,256]{2,3,1,0:T(8,128)S(1)} %collective-permute-done.1) | copy-start | bytes 393220
  24.5 9.3 %collective-permute-start.2 = (f32[2,2,320,32]{2,3,1,0:T(8,128)S(1)}, f32[2,2,320,32]{2,3,1,0:T(8,128)S(1)}, u32[]{:S(2)}, u32[]{:S(2)}) collective-permute-start(f32[2,2,320,32]{2,3,1,0:T(8,128)S(1)} %get-tuple-element.84), channel_id=1, source_target_pairs={{0,1},{1,2},{2,3},{3,4},{4,5},{5,6},{6,7},{7,8},{8,9},{9,10},{10,1... | collective-permute-start | bytes 491528 | tf_op jit(solution)/shard_map/ppermute | solution.py:25
  28.7 11.2 %collective-permute-start.3 = (f32[2,2,320,32]{2,3,1,0:T(8,128)S(1)}, f32[2,2,320,32]{2,3,1,0:T(8,128)S(1)}, u32[]{:S(2)}, u32[]{:S(2)}) collective-permute-start(f32[2,2,320,32]{2,3,1,0:T(8,128)S(1)} %get-tuple-element.85), channel_id=1, source_target_pairs={{1,0},{2,1},{3,2},{4,3},{5,4},{6,5},{7,6},{8,7},{9,8},{10,9},{11,1... | collective-permute-start | bytes 491528 | tf_op jit(solution)/shard_map/ppermute | solution.py:27
  41.8 1.3 copy-start
  45.4 1.9 copy-start.1
  47.3 1.3 copy-start
  50.9 1.9 copy-start.1
  53.1 6.6 %copy-start.6 = (f32[256,256]{0,1:T(8,128)S(1)}, f32[256,256]{0,1:T(8,128)}, u32[]{:S(2)}) copy-start(f32[256,256]{0,1:T(8,128)} %copy.64) | copy-start | bytes 786436
  53.1 6.6 %copy-start.7 = (f32[256,256]{0,1:T(8,128)S(1)}, f32[256,256]{0,1:T(8,128)}, u32[]{:S(2)}) copy-start(f32[256,256]{0,1:T(8,128)} %copy.71) | copy-start | bytes 786436
  53.1 6.6 %copy-start.8 = (f32[2,2,2,256,256]{3,4,0,2,1:T(8,128)S(1)}, f32[2,2,2,256,256]{3,4,0,2,1:T(8,128)}, u32[]{:S(2)}) copy-start(f32[2,2,2,256,256]{3,4,0,2,1:T(8,128)} %get-tuple-element.57) | copy-start | bytes 6291460
  95.9 5.5 %copy-start.4 = (f32[1,1,2,256,256]{3,4,2,1,0:T(8,128)S(1)}, f32[1,1,2,256,256]{3,4,2,1,0:T(8,128)}, u32[]{:S(2)}) copy-start(f32[1,1,2,256,256]{3,4,2,1,0:T(8,128)} %copy.98) | copy-start | bytes 1572868
  148.6 1.3 copy-start.5
  180.6 5.0 %copy-start.13 = (f32[256,256]{0,1:T(8,128)S(1)}, f32[256,256]{0,1:T(8,128)}, u32[]{:S(2)}) copy-start(f32[256,256]{0,1:T(8,128)} %get-tuple-element.66) | copy-start | bytes 786436
  180.6 5.0 %copy-start.14 = (f32[256,256]{0,1:T(8,128)S(1)}, f32[256,256]{0,1:T(8,128)}, u32[]{:S(2)}) copy-start(f32[256,256]{0,1:T(8,128)} %get-tuple-element.67) | copy-start | bytes 786436
  180.6 11.1 %collective-permute-start.4 = (f32[2,2,32,320]{3,2,1,0:T(8,128)S(1)}, f32[2,2,32,320]{3,2,1,0:T(8,128)}, u32[]{:S(2)}, u32[]{:S(2)}) collective-permute-start(f32[2,2,32,320]{3,2,1,0:T(8,128)S(1)} %copy.124), channel_id=1, source_target_pairs={{16,0},{17,1},{18,2},{19,3},{20,4},{21,5},{22,6},{23,7},{24,8},{25... | collective-permute-start | bytes 491528 | tf_op jit(solution)/shard_map/ppermute | solution.py:14
  187.3 9.4 %collective-permute-start.5 = (f32[2,2,32,320]{3,2,1,0:T(8,128)}, f32[2,2,32,320]{3,2,1,0:T(8,128)}, u32[]{:S(2)}, u32[]{:S(2)}) collective-permute-start(f32[2,2,32,320]{3,2,1,0:T(8,128)} %copy.126), channel_id=1, source_target_pairs={{0,16},{1,17},{2,18},{3,19},{4,20},{5,21},{6,22},{7,23},{8,24},{9,... | collective-permute-start | bytes 491528 | tf_op jit(solution)/shard_map/ppermute | solution.py:14
  199.0 118.7 %copy-start.11 = (f32[2,256,256]{1,2,0:T(8,128)S(1)}, f32[2,256,256]{1,2,0:T(8,128)}, u32[]{:S(2)}) copy-start(f32[2,256,256]{1,2,0:T(8,128)} %copy.129) | copy-start | bytes 1572868
  205.7 113.2 %collective-permute-start.6 = (f32[2,2,32,256]{3,2,1,0:T(8,128)}, f32[2,2,32,256]{3,2,1,0:T(8,128)S(1)}, u32[]{:S(2)}, u32[]{:S(2)}) collective-permute-start(f32[2,2,32,256]{3,2,1,0:T(8,128)} %get-tuple-element.91), channel_id=1, source_target_pairs={{1,0},{2,1},{3,2},{4,3},{5,4},{6,5},{7,6},{8,7},{9,8},{10,9},{11,1... | collective-permute-start | bytes 393224 | tf_op jit(solution)/shard_map/ppermute | solution.py:14
  207.0 154.9 %copy-start.3 = (f32[2,2,256,256]{2,3,1,0:T(8,128)S(1)}, f32[2,2,256,256]{2,3,1,0:T(8,128)}, u32[]{:S(2)}) copy-start(f32[2,2,256,256]{2,3,1,0:T(8,128)} %copy-done.2) | copy-start | bytes 3145732
  207.0 112.8 %collective-permute-start.7 = (f32[2,2,32,256]{3,2,1,0:T(8,128)S(1)}, f32[2,2,32,256]{3,2,1,0:T(8,128)S(1)}, u32[]{:S(2)}, u32[]{:S(2)}) collective-permute-start(f32[2,2,32,256]{3,2,1,0:T(8,128)S(1)} %get-tuple-element.90), channel_id=1, source_target_pairs={{0,1},{1,2},{2,3},{3,4},{4,5},{5,6},{6,7},{7,8},{8,9},{9,10},{10,1... | collective-permute-start | bytes 393224 | tf_op jit(solution)/shard_map/ppermute | solution.py:14
Sparse Core Ops, SparseCore 0:
  186.5 131.1 all-reduce.1
where the time goes:
time: 378 us; the launch traced here: 373 us
  waiting for transfers between devices  116 us (31%)
  matrix products  94.9 us (25%)
  local copies, waits for them, and re-layouts  67.4 us (18%)
  blocking collectives  39.5 us (10%)
  starting transfers between devices  21 us (6%)
  between operations  20.6 us (5%)
  other arithmetic  12.9 us (3%)
    psum x1, waiting for transfers between devices, local(): probe_total = lax.psum(probe_grad, ('row', 'col'))  106 us
    pmax x1, blocking collectives, local(): largest = lax.pmax(local_peak, ('row', 'col'))  39.5 us
    dynamic_update_slice x2, local copies, waits for them, and re-layouts, tile_gradient(): lax.dynamic_update_slice(gradient, current + pieces[position], start_at)  27.7 us
    dot_general x6, matrix products, transform(): ic = jnp.einsum('byx,xk->byk', imag_part, cosine, precision=high)  13.1 us
    dot_general x6, matrix products, transform(): rc = jnp.einsum('byx,xk->byk', real_part, cosine, precision=high)  12.6 us
    dot_general x6, matrix products, transform(): jnp.einsum('ky,byx->bkx', sine_tab, mid_im, precision=high)  12.4 us
    dot_general x6, matrix products, transform(): rs = jnp.einsum('byx,xk->byk', real_part, sine_tab, precision=high)  11.8 us
    ppermute x4, starting transfers between devices, passed_along(): lax.ppermute(value, axis, [(source, source + steps) for source in range(i...  11.8 us
  transfers between devices with their start and end apart: 9, of which 3 were waited for; matrix products, arithmetic and copies ran while one was open for 7% of the time, Pallas kernels for 0%

commit v1 on v0

v1 whole, which is shorter than its diff:
```python
import functools
import math

import jax
import jax.numpy as jnp
import numpy as np
from jax import lax
from jax.experimental import pallas as pl
from jax.experimental.pallas import tpu as pltpu
from jax.sharding import PartitionSpec as P

RIM = 32
LANES = 128
PLANES = 4
VMEM = pl.BlockSpec(memory_space=pltpu.VMEM)
SMEM = pl.BlockSpec(memory_space=pltpu.SMEM)
f32 = jnp.float32
bf16 = jnp.bfloat16


def split_np(table):
    high = table.astype(np.float32).astype(jnp.bfloat16)
    low = (table - high.astype(np.float64)).astype(np.float32).astype(jnp.bfloat16)
    return high, low


def tables(extent):
    line = np.arange(extent)
    angle = (np.outer(line, line) % extent) * (2.0 * math.pi / extent)
    cosine = np.cos(angle) / math.sqrt(extent)
    sine = np.sin(angle) / math.sqrt(extent)
    frequency = (line + extent // 2) % extent - extent // 2
    kernel = np.exp(-1j * math.pi * 8.0 / (extent * extent) * frequency.astype(np.float64) ** 2)
    forward = cosine - 1j * sine
    travel = (np.conj(forward) * kernel[None, :]) @ forward
    parts = []
    for table in (travel.real, travel.imag, cosine, sine):
        parts.extend(split_np(table))
    return np.stack(parts)


def split(value):
    high = value.astype(bf16)
    low = (value - high.astype(f32)).astype(bf16)
    return high, low


def lanes_of(rows):
    return lax.broadcasted_iota(jnp.int32, (rows, LANES), 1)


def pack_kernel(par, obj, col1, col2, *row_msgs):
    extent = obj.shape[-1]
    lane = lanes_of(extent)
    left = jnp.zeros((extent, LANES), f32)
    right = jnp.zeros((extent, LANES), f32)
    for q in range(PLANES):
        inside = (lane >= RIM * q) & (lane < RIM * (q + 1))
        head = obj[q, :, :LANES]
        tail = obj[q, :, extent - LANES :]
        head = pltpu.roll(head, RIM * q, 1) if q else head
        tail = pltpu.roll(tail, (RIM * q + RIM) % LANES, 1) if (RIM * q + RIM) % LANES else tail
        left = jnp.where(inside, head, left)
        right = jnp.where(inside, tail, right)
    odd_col = par[1] == 1
    col1[...] = jnp.where(odd_col, left, right)
    col2[...] = jnp.where(odd_col, right, left)
    for n, msg in enumerate(row_msgs):
        at_top = (par[0] + n) % 2
        start = pl.multiple_of((1 - at_top) * (extent - RIM), RIM)
        for q in range(PLANES):
            msg[RIM * q : RIM * (q + 1), :] = obj[q, pl.ds(start, RIM), :]


def tile_kernel(sides, pos, par, obj, col1, col2, *rest):
    row_in = rest[:sides]
    corner_in = rest[sides : 2 * sides]
    probe, measured, tabs = rest[2 * sides : 2 * sides + 3]
    outs = rest[2 * sides + 3 :]
    row_out = outs[:sides]
    keep_out, inner_out, left_out, right_out = outs[sides : sides + 4]
    window, grad, patch, wave, mats, right_in, left_in = outs[sides + 4 :]
    extent = obj.shape[-1]
    tiles = extent // LANES
    count = pos.shape[0]
    span = extent + 2 * RIM
    lane = lanes_of(extent)
    odd_row = par[0]
    odd_col = par[1] == 1

    for part in range(2):
        a_re, a_im, cosine, sine = (tabs[2 * t + part] for t in range(4))
        for index, diag, upper, lower in (
            (0, a_re, a_im, -a_im),
            (1, a_re, -a_im, a_im),
            (2, cosine, -sine, sine),
            (3, cosine, sine, -sine),
        ):
            mats[index, part, :extent, :extent] = diag
            mats[index, part, extent:, extent:] = diag
            mats[index, part, :extent, extent:] = upper
            mats[index, part, extent:, :extent] = lower

    rim1 = col1[...]
    rim2 = col2[...]
    from_left = jnp.where(odd_col, rim1, rim2)
    from_right = jnp.where(odd_col, rim2, rim1)
    if sides == 1:
        start = pl.multiple_of(odd_row * (extent + RIM), RIM)
        for q in range(PLANES):
            for t in range(tiles + 2):
                window[q, t, pl.ds(start, RIM), :] = jnp.zeros((RIM, LANES), f32)
    starts = [pl.multiple_of((1 - (odd_row + n) % 2) * (extent + RIM), RIM) for n in range(sides)]
    for q in range(PLANES):
        turn_left = (LANES - RIM - RIM * q) % LANES
        turn_right = (LANES - RIM * q) % LANES
        turned = lambda value, turn: pltpu.roll(value, turn, 1) if turn else value
        window[q, 0, RIM : RIM + extent, :] = turned(from_left, turn_left)
        window[q, tiles + 1, RIM : RIM + extent, :] = turned(from_right, turn_right)
        for t in range(tiles):
            window[q, t + 1, RIM : RIM + extent, :] = obj[q, :, LANES * t : LANES * (t + 1)]
        for n in range(sides):
            corner1 = corner_in[n][:RIM, :]
            corner2 = corner_in[n][RIM:, :]
            window[q, 0, pl.ds(starts[n], RIM), :] = turned(jnp.where(odd_col, corner1, corner2), turn_left)
            window[q, tiles + 1, pl.ds(starts[n], RIM), :] = turned(jnp.where(odd_col, corner2, corner1), turn_right)
            for t in range(tiles):
                window[q, t + 1, pl.ds(starts[n], RIM), :] = row_in[n][RIM * q : RIM * (q + 1), LANES * t : LANES * (t + 1)]

    for q in range(PLANES):
        for t in range(tiles + 2):
            grad[q, t] = jnp.zeros((span, LANES), f32)

    def place(p):
        across = pos[p, 1] + LANES
        return pos[p, 0] + RIM, across // LANES, across % LANES

    def cols(c):
        return slice(c * extent, (c + 1) * extent)

    def to_right(p, re, im):
        for c, value in ((0, re), (1, im)):
            high, low = split(value)
            right_in[0, cols(p), cols(c)] = high
            right_in[1, cols(p), cols(c)] = low

    def right_stage(index):
        for p in range(count):
            for c in range(2):
                first = jnp.dot(right_in[0, cols(p), :], mats[index, 0, :, cols(c)], preferred_element_type=f32)
                first += jnp.dot(right_in[0, cols(p), :], mats[index, 1, :, cols(c)], preferred_element_type=f32)
                first += jnp.dot(right_in[1, cols(p), :], mats[index, 0, :, cols(c)], preferred_element_type=f32)
                high, low = split(first)
                left_in[0, cols(c), cols(p)] = high
                left_in[1, cols(c), cols(p)] = low

    def left_stage(index, p):
        out = []
        for c in range(2):
            first = jnp.dot(mats[index, 0, cols(c), :], left_in[0, :, cols(p)], preferred_element_type=f32)
            first += jnp.dot(mats[index, 1, cols(c), :], left_in[0, :, cols(p)], preferred_element_type=f32)
            first += jnp.dot(mats[index, 0, cols(c), :], left_in[1, :, cols(p)], preferred_element_type=f32)
            out.append(first)
        return out

    def add_piece(p, q, value):
        down, first, turn = place(p)
        moved = [pltpu.roll(value[:, LANES * t : LANES * (t + 1)], turn, 1) for t in range(tiles)]
        for t in range(tiles + 1):
            if t == 0:
                piece = jnp.where(lane >= turn, moved[0], 0.0)
            elif t == tiles:
                piece = jnp.where(lane >= turn, 0.0, moved[t - 1])
            else:
                piece = jnp.where(lane >= turn, moved[t], moved[t - 1])
            grad[q, first + t, pl.ds(down, extent), :] += piece

    for p in range(count):
        down, first, turn = place(p)
        back = (LANES - turn) % LANES
        for q in range(PLANES):
            got = [pltpu.roll(window[q, first + t, pl.ds(down, extent), :], back, 1) for t in range(tiles + 1)]
            for t in range(tiles):
                patch[p, q, :, LANES * t : LANES * (t + 1)] = jnp.where(lane < LANES - turn, got[t], got[t + 1])
        pr, pi = probe[0], probe[1]
        ar, ai = patch[p, 0], patch[p, 1]
        to_right(p, pr * ar - pi * ai, pr * ai + pi * ar)
    right_stage(0)
    for p in range(count):
        qr, qi = left_stage(1, p)
        wave[p, 0] = qr
        wave[p, 1] = qi
        br, bi = patch[p, 2], patch[p, 3]
        to_right(p, qr * br - qi * bi, qr * bi + qi * br)
    right_stage(2)
    for p in range(count):
        fr, fi = left_stage(3, p)
        excess = 2.0 * (fr * fr + fi * fi - measured[p])
        to_right(p, excess * fr, excess * fi)
    right_stage(3)
    for p in range(count):
        hr, hi = left_stage(2, p)
        qr, qi = wave[p, 0], wave[p, 1]
        add_piece(p, 2, qr * hr + qi * hi)
        add_piece(p, 3, qr * hi - qi * hr)
        br, bi = patch[p, 2], patch[p, 3]
        to_right(p, br * hr + bi * hi, br * hi - bi * hr)
    right_stage(1)
    total_re = total_im = None
    for p in range(count):
        er, ei = left_stage(0, p)
        pr, pi = probe[0], probe[1]
        add_piece(p, 0, pr * er + pi * ei)
        add_piece(p, 1, pr * ei - pi * er)
        ar, ai = patch[p, 0], patch[p, 1]
        gr = ar * er + ai * ei
        gi = ar * ei - ai * er
        if p:
            gr = wave[0, 0] + gr
            gi = wave[0, 1] + gi
        wave[0, 0] = gr
        wave[0, 1] = gi
    is_odd = odd_row == 1
    keep_out[...] = jnp.where(is_odd, wave[0, 1], wave[0, 0])
    row_out[0][:extent, :] = jnp.where(is_odd, wave[0, 0], wave[0, 1])

    def packed(tile, left, start, rows):
        out = jnp.zeros((rows, LANES), f32)
        narrow = lanes_of(rows)
        for q in range(PLANES):
            value = grad[q, tile, pl.ds(start, rows), :]
            turn = (RIM * q + (RIM if left else 0)) % LANES
            value = pltpu.roll(value, turn, 1) if turn else value
            out = jnp.where((narrow >= RIM * q) & (narrow < RIM * (q + 1)), value, out)
        return out

    left_out[...] = packed(0, True, RIM, extent)
    right_out[...] = packed(tiles + 1, False, RIM, extent)
    for q in range(PLANES):
        for t in range(tiles):
            inner_out[q, :, LANES * t : LANES * (t + 1)] = grad[q, t + 1, RIM : RIM + extent, :]
    for n in range(sides):
        base = extent if n == 0 else 0
        for q in range(PLANES):
            for t in range(tiles):
                row_out[n][base + RIM * q : base + RIM * (q + 1), LANES * t : LANES * (t + 1)] = grad[q, t + 1, pl.ds(starts[n], RIM), :]
        at = base + RIM * PLANES
        row_out[n][at : at + RIM, :LANES] = packed(0, True, starts[n], RIM)
        row_out[n][at : at + RIM, LANES : 2 * LANES] = packed(tiles + 1, False, starts[n], RIM)


def cols_kernel(sides, par, keep, left, right, *rest):
    row_in = rest[:sides]
    msg1, msg2, keep2, edge = rest[sides:]
    extent = left.shape[0]
    half = extent // 2
    odd_col = par[1] == 1
    for n in range(sides):
        base = (extent if n == 0 else 0) + RIM * PLANES
        start = pl.multiple_of((1 - (par[0] + n) % 2) * (extent - RIM), RIM)
        if n == 0:
            edge[0] = left[...]
            edge[1] = right[...]
        for s in range(2):
            edge[s, pl.ds(start, RIM), :] += row_in[n][base : base + RIM, LANES * s : LANES * (s + 1)]
    to1 = jnp.where(odd_col, edge[0], edge[1])
    to2 = jnp.where(odd_col, edge[1], edge[0])
    lower = keep[:half, :] + row_in[0][:half, :]
    upper = keep[half:, :] + row_in[0][half:extent, :]
    keep2[...] = jnp.where(odd_col, upper, lower)
    msg1[:half, :] = jnp.where(odd_col, lower, upper)
    msg1[half:, :LANES] = to1[:half]
    msg1[half:, LANES:] = to1[half:]
    msg2[:, :LANES] = to2[:half]
    msg2[:, LANES:] = to2[half:]


def gather_kernel(sides, par, inner, keep3, got3, col1, col2, *rest):
    row_in = rest[:sides]
    msg, descent = rest[sides:]
    extent = inner.shape[-1]
    half = extent // 2
    quarter = keep3.shape[0]
    tiles = extent // LANES
    odd_col = par[1] == 1
    lane = lanes_of(half)
    descent[...] = inner[...]
    for n in range(sides):
        base = extent if n == 0 else 0
        start = pl.multiple_of((1 - (par[0] + n) % 2) * (extent - RIM), RIM)
        for q in range(PLANES):
            descent[q, pl.ds(start, RIM), :] += row_in[n][base + RIM * q : base + RIM * (q + 1), :]
    for s in range(2):
        rim1 = col1[half:, LANES * s : LANES * (s + 1)]
        rim2 = col2[:, LANES * s : LANES * (s + 1)]
        from_left = jnp.where(odd_col, rim1, rim2)
        from_right = jnp.where(odd_col, rim2, rim1)
        rows = slice(half * s, half * (s + 1))
        for q in range(PLANES):
            turn_left = (LANES - RIM * q) % LANES
            turn_right = (LANES - RIM - RIM * q) % LANES
            on_left = pltpu.roll(from_left, turn_left, 1) if turn_left else from_left
            on_right = pltpu.roll(from_right, turn_right, 1) if turn_right else from_right
            descent[q, rows, :LANES] += jnp.where(lane < RIM, on_left, 0.0)
            descent[q, rows, extent - LANES :] += jnp.where(lane >= LANES - RIM, on_right, 0.0)
    peak = None
    for s in range(2):
        power = descent[2 * s] * descent[2 * s] + descent[2 * s + 1] * descent[2 * s + 1]
        power = jnp.max(power.reshape(extent // 8, 8, extent), axis=0)
        peak = power if peak is None else jnp.maximum(peak, power)
    msg[:quarter, :] = keep3[...] + got3[...]
    msg[quarter:, :] = peak


def final_kernel(rate, par, obj, descent, probe, mine, other, obj_out, probe_out):
    extent = obj.shape[-1]
    odd_row = par[0] == 1
    peak = jnp.max(jnp.maximum(mine[extent:, :], other[extent:, :]))
    peak = jnp.broadcast_to(peak, (8, extent))
    scale = (0.3 / (jnp.sqrt(peak) + 1e-06))[:1, :]
    for q in range(PLANES):
        obj_out[q] = obj[q] - descent[q] * scale
    probe_out[0] = probe[0] - rate * jnp.where(odd_row, other[:extent, :], mine[:extent, :])
    probe_out[1] = probe[1] - rate * jnp.where(odd_row, mine[:extent, :], other[:extent, :])


def call(kernel, outs, ins, scratch=(), smem=1, name=None):
    return pl.pallas_call(
        kernel,
        out_shape=tuple(jax.ShapeDtypeStruct(shape, f32) for shape in outs),
        in_specs=[SMEM] * smem + [VMEM] * (len(ins) - smem),
        out_specs=tuple(VMEM for _ in outs),
        scratch_shapes=list(scratch),
        compiler_params=pltpu.CompilerParams(vmem_limit_bytes=48 * 1024 * 1024),
        name=name,
    )(*ins)


def swap(value, axis, bit):
    count = lax.axis_size(axis)
    return lax.ppermute(value, axis, [(i, i ^ bit) for i in range(count)])


def pairs(value, axis, phase):
    count = lax.axis_size(axis)
    links = []
    for i in range(phase, count - 1, 2):
        links += [(i, i + 1), (i + 1, i)]
    return lax.ppermute(value, axis, links)


def local(object_in, probe_in, positions, intensity):
    extent = probe_in.shape[-1]
    half, quarter = extent // 2, extent // 4
    rows, cols = lax.axis_size("row"), lax.axis_size("col")
    sides = 1 if rows == 2 else 2
    row, col = lax.axis_index("row"), lax.axis_index("col")
    par = jnp.stack([row % 2, col % 2]).astype(jnp.int32)
    offsets = positions.reshape(-1, 2)
    count = offsets.shape[0]
    measured = intensity.reshape(-1, extent, extent)
    obj = object_in.reshape(PLANES, extent, extent)
    tabs = jnp.asarray(tables(extent))

    sent = call(pack_kernel, [(extent, LANES)] * 2 + [(PLANES * RIM, extent)] * sides, (par, obj), name="pack")
    col2 = pairs(sent[1], "col", 1)
    col1 = pairs(sent[0], "col", 0)
    row_in = [pairs(sent[2 + n], "row", n) for n in range(sides)]
    corner_in = []
    for n in range(sides):
        start = jnp.where((row + n) % 2 == 0, extent - RIM, 0)
        corner = jnp.concatenate([lax.dynamic_slice_in_dim(c, start, RIM, 0) for c in (col1, col2)], 0)
        corner_in.append(pairs(corner, "row", n))

    span = extent + 2 * RIM
    tiles = extent // LANES
    rim_rows = RIM * (PLANES + 1)
    wide = (2 * extent, 2 * extent)
    out = call(
        functools.partial(tile_kernel, sides),
        [(extent + rim_rows, extent)] + [(rim_rows, extent)] * (sides - 1)
        + [(extent, extent), (PLANES, extent, extent), (extent, LANES), (extent, LANES)],
        (offsets, par, obj, col1, col2, *row_in, *corner_in, probe_in, measured, tabs),
        scratch=[
            pltpu.VMEM((PLANES, tiles + 2, span, LANES), f32),
            pltpu.VMEM((PLANES, tiles + 2, span, LANES), f32),
            pltpu.VMEM((count, PLANES, extent, extent), f32),
            pltpu.VMEM((count, 2, extent, extent), f32),
            pltpu.VMEM((4, 2) + wide, bf16),
            pltpu.VMEM((2, count * extent, 2 * extent), bf16),
            pltpu.VMEM((2, 2 * extent, count * extent), bf16),
        ],
        smem=2,
        name="tile",
    )
    row_back = [pairs(out[n], "row", n) for n in range(sides)]
    keep, inner, left, right = out[sides:]
    msg1, msg2, keep2 = call(
        functools.partial(cols_kernel, sides),
        [(extent, extent), (half, extent), (half, extent)],
        (par, keep, left, right, *row_back),
        scratch=[pltpu.VMEM((2, extent, LANES), f32)],
        name="cols",
    )
    got1 = pairs(msg1, "col", 0)
    got2 = pairs(msg2, "col", 1)
    both = keep2 + got1[:half]
    up = (col // 2) % 2 == 1
    keep3 = jnp.where(up, both[quarter:], both[:quarter])
    got3 = swap(jnp.where(up, both[:quarter], both[quarter:]), "col", 2)
    state, descent = call(
        functools.partial(gather_kernel, sides),
        [(quarter + 8, extent), (PLANES, extent, extent)],
        (par, inner, keep3, got3, got1, got2, *row_back),
        name="gather",
    )
    is_sum = lax.broadcasted_iota(jnp.int32, state.shape, 0) < quarter
    steps = [("col", 1 << b) for b in range(2, cols.bit_length() - 1)]
    steps += [("row", 1 << b) for b in range(1, rows.bit_length() - 1)]
    for axis, bit in steps:
        other = swap(state, axis, bit)
        state = jnp.where(is_sum, state + other, jnp.maximum(state, other))

    def joined(state, other, up):
        top = state.shape[0] - 8
        low = jnp.where(up, other[:top], state[:top])
        high = jnp.where(up, state[:top], other[:top])
        return jnp.concatenate([low, high, jnp.maximum(state[top:], other[top:])], 0)

    state = joined(state, swap(state, "col", 2), up)
    state = joined(state, swap(state, "col", 1), col % 2 == 1)
    other = swap(state, "row", 1)
    object_out, probe_out = call(
        functools.partial(final_kernel, 2.0 / (rows * cols)),
        [obj.shape, probe_in.shape],
        (par, obj, descent, probe_in, state, other),
        name="final",
    )
    return object_out.reshape(object_in.shape), probe_out


def solution(mesh):
    placed = (
        P(None, None, "row", "col"),
        P(),
        P("row", "col", None, None),
        P("row", "col", None, None, None),
    )
    return jax.shard_map(
        local,
        mesh=mesh,
        in_specs=placed,
        out_specs=(P(None, None, "row", "col"), P()),
        check_vma=False,
    )
```

time: 378 us -> 71.1 us (0.19); the launches traced: 373 us -> 70.7 us
  matrix products: 94.9 us -> 0 us
  waiting for transfers between devices: 116 us -> 29.7 us
  local copies, waits for them, and re-layouts: 67.4 us -> 6.19 us
  blocking collectives: 39.5 us -> 0 us
  between operations: 20.6 us -> 0.82 us
  Pallas kernels: 0 us -> 13.7 us
  other arithmetic: 12.9 us -> 0.35 us
    psum x1 -> x0, waiting for transfers between devices: 106 us -> none  [local(): probe_total = lax.psum(probe_grad, ('row', 'col'))]
    dot_general x48 -> x0, matrix products: 94.9 us -> none  [the longest x6 13.1 us: transform(): ic = jnp.einsum('byx,xk->byk', imag_part, cosine, precision=high)]
    pmax x1 -> x0, blocking collectives: 39.5 us -> none  [local(): largest = lax.pmax(local_peak, ('row', 'col'))]
    dynamic_update_slice x2 -> x0, local copies, waits for them, and re-layouts: 27.7 us -> none  [tile_gradient(): lax.dynamic_update_slice(gradient, current + pieces[position], start_at)]
    ppermute x8 -> x13, waiting for transfers between devices: 9.87 us -> 29.7 us  [the longest x6 16 us: swap(): return lax.ppermute(value, axis, [(i, i ^ bit) for i in range(count)])]
    pallas_call x0 -> x5, Pallas kernels: none -> 13.7 us  [call(): pl.pallas_call(kernel, out_shape=tuple((jax.ShapeDtypeStruct(shape, f32)...]
    gather x20 -> x0, local copies, waits for them, and re-layouts: 11 us -> none
    scatter-add x2 -> x0, local copies, waits for them, and re-layouts: 7.4 us -> none  [the longest x1 3.75 us: rows_then_cols(): middle = middle.at[:, :, inner_px - RIM:, :].add(from_below)]
  transfers between devices with their start and end apart: 9 -> 13, of which waited for: 3 -> 10; matrix products, arithmetic and copies ran while one was open for 7% -> 0% of each run, Pallas kernels for 0% -> 0%
where the time goes in v1:
time: 71.1 us; the launch traced here: 70.7 us
  waiting for transfers between devices  29.7 us (42%)
  starting transfers between devices  20 us (28%)
  Pallas kernels  13.7 us (19%)
  local copies, waits for them, and re-layouts  6.19 us (9%)
  between operations  0.82 us (1%)
    ppermute x6, waiting for transfers between devices, swap(): return lax.ppermute(value, axis, [(i, i ^ bit) for i in range(count)])  16 us
    ppermute x7, waiting for transfers between devices, pairs(): return lax.ppermute(value, axis, links)  13.7 us
    pallas_call x5, Pallas kernels, call(): pl.pallas_call(kernel, out_shape=tuple((jax.ShapeDtypeStruct(shape, f32)...  13.7 us
    ppermute x7, starting transfers between devices, pairs(): return lax.ppermute(value, axis, links)  10.1 us
    ppermute x6, starting transfers between devices, swap(): return lax.ppermute(value, axis, [(i, i ^ bit) for i in range(count)])  9.84 us
    unnamed x18, local copies, waits for them, and re-layouts  6.18 us
  transfers between devices with their start and end apart: 13, of which 10 were waited for; matrix products, arithmetic and copies ran while one was open for 0% of the time, Pallas kernels for 0%

profile of v1, /device:TPU:0, one launch (start us, length us, event | category | flops | bytes accessed | tf_op | source)
XLA Modules:
  0.0 70.7 jit_solution(17388079885649202315)
XLA Ops:
  0.6 0.1 pad_add_fusion.par
  0.7 0.0 copy-start
  0.7 1.2 %copy-done = f32[2,2,256,256]{3,2,1,0:T(8,128)S(1)} copy-done((f32[2,2,256,256]{3,2,1,0:T(8,128)S(1)}, f32[2,2,256,256]{3,2,1,0:T(8,128)}, u32[]{:S(2)}) %copy-start) | copy-done | bytes 1048600
  2.0 0.0 copy-start.1
  2.0 0.8 %pack.1 = (f32[256,128]{1,0:T(8,128)S(1)}, f32[256,128]{1,0:T(8,128)S(1)}, f32[128,256]{1,0:T(8,128)S(1)}) custom-call(s32[2]{0:T(128)S(1)} %pad_add_fusion.par, f32[4,256,256]{2,1,0:T(8,128)S(1)} %bitcast.6), custom_call_target="tpu_custom_call" | custom-call | tf_op jit(solution)/shard_map/pack/pallas_call | solution.py:328
  2.8 3.0 %collective-permute-start = (f32[256,128]{1,0:T(8,128)S(1)}, f32[256,128]{1,0:T(8,128)S(1)}, u32[]{:S(2)}, u32[]{:S(2)}) collective-permute-start(f32[256,128]{1,0:T(8,128)S(1)} %get-tuple-element.17), channel_id=1, source_target_pairs={{0,1},{1,0},{2,3},{3,2},{4,5},{5,4},{6,7},{7,6},{8,9},{9,8},{10,11... | collective-permute-start | bytes 393224 | tf_op jit(solution)/shard_map/ppermute | solution.py:349
  5.8 0.7 collective-permute-start.1
  6.5 0.1 collective-permute-start.2
  6.6 2.7 %collective-permute-done.col1 = f32[256,128]{1,0:T(8,128)S(1)} collective-permute-done((f32[256,128]{1,0:T(8,128)S(1)}, f32[256,128]{1,0:T(8,128)S(1)}, u32[]{:S(2)}, u32[]{:S(2)}) %collective-permute-start) | collective-permute-done | bytes 131104 | tf_op jit(solution)/shard_map/ppermute | solution.py:349
  9.3 0.0 collective-permute-done.1.col2
  9.3 0.1 collective-permute-start.3
  9.4 0.0 collective-permute-done.2.rest_0_
  9.4 1.2 %collective-permute-done.3.rest_1_ = f32[64,128]{1,0:T(8,128)S(1)} collective-permute-done((f32[64,128]{1,0:T(8,128)S(1)}, f32[64,128]{1,0:T(8,128)S(1)}, u32[]{:S(2)}, u32[]{:S(2)}) %collective-permute-start.3) | collective-permute-done | bytes 32800 | tf_op jit(solution)/shard_map/ppermute | solution.py:349
  10.6 0.0 copy-start.8
  10.6 0.0 copy-done.1
  10.6 0.7 copy-done.8
  11.3 0.0 copy-start.2
  11.3 1.0 %copy-done.2 = f32[2,256,256]{2,1,0:T(8,128)S(1)} copy-done((f32[2,256,256]{2,1,0:T(8,128)S(1)}, f32[2,256,256]{2,1,0:T(8,128)}, u32[]{:S(2)}) %copy-start.2) | copy-done | bytes 524312
  12.3 1.2 %copy-done.6 = bf16[8,256,256]{2,1,0:T(8,128)(2,1)S(1)} copy-done((bf16[8,256,256]{2,1,0:T(8,128)(2,1)S(1)}, bf16[8,256,256]{2,1,0:T(8,128)(2,1)}, u32[]{:S(2)}) %copy-start.6) | copy-done | bytes 1048600
  13.6 1.0 %copy-done.7 = f32[1,1,2,256,256]{4,3,2,1,0:T(8,128)S(1)} copy-done((f32[1,1,2,256,256]{4,3,2,1,0:T(8,128)S(1)}, f32[1,1,2,256,256]{4,3,2,1,0:T(8,128)}, u32[]{:S(2)}) %copy-start.7) | copy-done | bytes 524312
  14.6 9.3 %tile.1 = (f32[416,256]{1,0:T(8,128)S(1)}, f32[256,256]{1,0:T(8,128)S(1)}, f32[4,256,256]{2,1,0:T(8,128)S(1)}, f32[256,128]{1,0:T(8,128)S(1)}, f32[256,128]{1,0:T(8,128)S(1)}) custom-call(s32[2,2]{1,0:T(2,128)S(1)} %bitcast.10, s32[2]{0:T(128)S(1)} %pad_add_fusion.par, f32[4,256,256]{2,1,0:T(8,128)S(1)} %bitcast.7, ...), custom_call_target="tpu_custom_call" | custom-call | tf_op jit(solution)/shard_map/tile/pallas_call | solution.py:328
  23.9 0.2 collective-permute-start.4
  24.1 1.6 %collective-permute-done.4.rest_0_ = f32[416,256]{1,0:T(8,128)S(1)} collective-permute-done((f32[416,256]{1,0:T(8,128)S(1)}, f32[416,256]{1,0:T(8,128)S(1)}, u32[]{:S(2)}, u32[]{:S(2)}) %collective-permute-start.4) | collective-permute-done | bytes 426016 | tf_op jit(solution)/shard_map/ppermute | solution.py:349
  25.7 0.6 cols.1
  26.4 5.5 %collective-permute-start.5 = (f32[256,256]{1,0:T(8,128)S(1)}, f32[256,256]{1,0:T(8,128)S(1)}, u32[]{:S(2)}, u32[]{:S(2)}) collective-permute-start(f32[256,256]{1,0:T(8,128)S(1)} %get-tuple-element.26), channel_id=1, source_target_pairs={{0,1},{1,0},{2,3},{3,2},{4,5},{5,4},{6,7},{7,6},{8,9},{9,8},{10,11... | collective-permute-start | bytes 786440 | tf_op jit(solution)/shard_map/ppermute | solution.py:349
  31.8 0.7 collective-permute-start.7
  32.5 8.1 %collective-permute-done.5.col1 = f32[256,256]{1,0:T(8,128)S(1)} collective-permute-done((f32[256,256]{1,0:T(8,128)S(1)}, f32[256,256]{1,0:T(8,128)S(1)}, u32[]{:S(2)}, u32[]{:S(2)}) %collective-permute-start.5) | collective-permute-done | bytes 262176 | tf_op jit(solution)/shard_map/ppermute | solution.py:349
  40.6 0.1 collective-permute-start.6
  40.7 0.0 collective-permute-done.7.col2
  40.7 4.2 %collective-permute-done.6.got3 = f32[64,256]{1,0:T(8,128)S(1)} collective-permute-done((f32[64,256]{1,0:T(8,128)S(1)}, f32[64,256]{1,0:T(8,128)S(1)}, u32[]{:S(2)}, u32[]{:S(2)}) %collective-permute-start.6) | collective-permute-done | bytes 65568 | tf_op jit(solution)/shard_map/ppermute | solution.py:341
  45.0 0.9 %gather.1 = (f32[72,256]{1,0:T(8,128)S(1)}, f32[4,256,256]{2,1,0:T(8,128)S(1)}) custom-call(s32[2]{0:T(128)S(1)} %pad_add_fusion.par, f32[4,256,256]{2,1,0:T(8,128)S(1)} %get-tuple-element.20.inner, f32[64,256]{1,0:T(8,128)S(1)} %get-tuple-element.37.keep3, f32[64,256]{1,0:T(8,128)S(1)} %collective-permute-done.6.got3, ...), custom_call_target="tpu_custom_call" | custom-call | tf_op jit(solution)/shard_map/gather/pallas_call | solution.py:328
  45.9 0.0 copy-start.4
  45.9 1.0 %copy-done.4 = f32[4,256,256]{2,1,0:T(8,128)} copy-done((f32[4,256,256]{2,1,0:T(8,128)}, f32[4,256,256]{2,1,0:T(8,128)S(1)}, u32[]{:S(2)}) %copy-start.4) | copy-done | bytes 1048600
  46.9 2.2 %collective-permute-start.8 = (f32[72,256]{1,0:T(8,128)S(1)}, f32[72,256]{1,0:T(8,128)S(1)}, u32[]{:S(2)}, u32[]{:S(2)}) collective-permute-start(f32[72,256]{1,0:T(8,128)S(1)} %get-tuple-element.29), channel_id=1, source_target_pairs={{0,4},{1,5},{2,6},{3,7},{4,0},{5,1},{6,2},{7,3},{8,12},{9,13},{10,... | collective-permute-start | bytes 221192 | tf_op jit(solution)/shard_map/ppermute | solution.py:341
  49.1 2.3 %collective-permute-done.8 = f32[72,256]{1,0:T(8,128)S(1)} collective-permute-done((f32[72,256]{1,0:T(8,128)S(1)}, f32[72,256]{1,0:T(8,128)S(1)}, u32[]{:S(2)}, u32[]{:S(2)}) %collective-permute-start.8) | collective-permute-done | bytes 73760 | tf_op jit(solution)/shard_map/ppermute | solution.py:341
  51.4 0.1 maximum_select_fusion.1
  51.5 3.3 %collective-permute-start.9 = (f32[72,256]{1,0:T(8,128)S(1)}, f32[72,256]{1,0:T(8,128)S(1)}, u32[]{:S(2)}, u32[]{:S(2)}) collective-permute-start(f32[72,256]{1,0:T(8,128)S(1)} %maximum_select_fusion.1), channel_id=1, source_target_pairs={{0,8},{1,9},{2,10},{3,11},{4,12},{5,13},{6,14},{7,15},{8,0},{9,1},... | collective-permute-start | bytes 221192 | tf_op jit(solution)/shard_map/ppermute | solution.py:341
  54.8 2.3 %collective-permute-done.9 = f32[72,256]{1,0:T(8,128)S(1)} collective-permute-done((f32[72,256]{1,0:T(8,128)S(1)}, f32[72,256]{1,0:T(8,128)S(1)}, u32[]{:S(2)}, u32[]{:S(2)}) %collective-permute-start.9) | collective-permute-done | bytes 73760 | tf_op jit(solution)/shard_map/ppermute | solution.py:341
  57.1 0.1 maximum_select_fusion
  57.2 2.4 %collective-permute-start.10 = (f32[72,256]{1,0:T(8,128)S(1)}, f32[72,256]{1,0:T(8,128)S(1)}, u32[]{:S(2)}, u32[]{:S(2)}) collective-permute-start(f32[72,256]{1,0:T(8,128)S(1)} %maximum_select_fusion), channel_id=1, source_target_pairs={{0,2},{1,3},{2,0},{3,1},{4,6},{5,7},{6,4},{7,5},{8,10},{9,11},{10,... | collective-permute-start | bytes 221192 | tf_op jit(solution)/shard_map/ppermute | solution.py:341
  59.6 2.3 %collective-permute-done.10 = f32[72,256]{1,0:T(8,128)S(1)} collective-permute-done((f32[72,256]{1,0:T(8,128)S(1)}, f32[72,256]{1,0:T(8,128)S(1)}, u32[]{:S(2)}, u32[]{:S(2)}) %collective-permute-start.10) | collective-permute-done | bytes 73760 | tf_op jit(solution)/shard_map/ppermute | solution.py:341
  61.9 1.8 %collective-permute-start.11 = (f32[136,256]{1,0:T(8,128)S(1)}, f32[136,256]{1,0:T(8,128)S(1)}, u32[]{:S(2)}, u32[]{:S(2)}) collective-permute-start(f32[136,256]{1,0:T(8,128)S(1)} %pad_maximum_fusion.1), channel_id=1, source_target_pairs={{0,1},{1,0},{2,3},{3,2},{4,5},{5,4},{6,7},{7,6},{8,9},{9,8},{10,11... | collective-permute-start | bytes 417800 | tf_op jit(solution)/shard_map/ppermute | solution.py:341
  63.8 3.3 %collective-permute-done.11 = f32[136,256]{1,0:T(8,128)S(1)} collective-permute-done((f32[136,256]{1,0:T(8,128)S(1)}, f32[136,256]{1,0:T(8,128)S(1)}, u32[]{:S(2)}, u32[]{:S(2)}) %collective-permute-start.11) | collective-permute-done | bytes 139296 | tf_op jit(solution)/shard_map/ppermute | solution.py:341
  67.1 0.1 collective-permute-start.12
  67.2 1.5 %collective-permute-done.12.other = f32[264,256]{1,0:T(8,128)S(1)} collective-permute-done((f32[264,256]{1,0:T(8,128)S(1)}, f32[264,256]{1,0:T(8,128)S(1)}, u32[]{:S(2)}, u32[]{:S(2)}) %collective-permute-start.12) | collective-permute-done | bytes 270368 | tf_op jit(solution)/shard_map/ppermute | solution.py:341
  68.7 0.0 copy-done.5
  68.7 0.0 copy-done.3
  68.7 2.0 %final.1 = (f32[4,256,256]{2,1,0:T(8,128)}, f32[2,256,256]{2,1,0:T(8,128)}) custom-call(s32[2]{0:T(128)S(1)} %pad_add_fusion.par, f32[4,256,256]{2,1,0:T(8,128)S(1)} %bitcast.8, f32[4,256,256]{2,1,0:T(8,128)S(1)} %copy-done.5, f32[2,256,256]{2,1,0:T(8,128)S(1)} %copy-done.3, f32[264,256]{1,0:T(8,128)S(1)} %pad_maximum_fusion.mine, ...), custom_call_target="tpu_custom_call" | custom-call | tf_op jit(solution)/shard_map/final/pallas_call | solution.py:328
  (16 shorter events, 0.1 us)
Async XLA Ops:
  0.7 1.2 %copy-start = (f32[2,2,256,256]{3,2,1,0:T(8,128)S(1)}, f32[2,2,256,256]{3,2,1,0:T(8,128)}, u32[]{:S(2)}) copy-start(f32[2,2,256,256]{3,2,1,0:T(8,128)} %param.5) | copy-start | bytes 3145732
  2.0 8.7 %copy-start.1 = (f32[2,2,256,256]{3,2,1,0:T(8,128)S(1)}, f32[2,2,256,256]{3,2,1,0:T(8,128)}, u32[]{:S(2)}) copy-start(f32[2,2,256,256]{3,2,1,0:T(8,128)} %param.5) | copy-start | bytes 3145732
  2.8 6.5 %collective-permute-start = (f32[256,128]{1,0:T(8,128)S(1)}, f32[256,128]{1,0:T(8,128)S(1)}, u32[]{:S(2)}, u32[]{:S(2)}) collective-permute-start(f32[256,128]{1,0:T(8,128)S(1)} %get-tuple-element.17), channel_id=1, source_target_pairs={{0,1},{1,0},{2,3},{3,2},{4,5},{5,4},{6,7},{7,6},{8,9},{9,8},{10,11... | collective-permute-start | bytes 393224 | tf_op jit(solution)/shard_map/ppermute | solution.py:349
  5.8 3.5 %collective-permute-start.1 = (f32[256,128]{1,0:T(8,128)S(1)}, f32[256,128]{1,0:T(8,128)S(1)}, u32[]{:S(2)}, u32[]{:S(2)}) collective-permute-start(f32[256,128]{1,0:T(8,128)S(1)} %get-tuple-element.18), channel_id=1, source_target_pairs={{1,2},{2,1},{3,4},{4,3},{5,6},{6,5},{7,8},{8,7},{9,10},{10,9},{11,... | collective-permute-start | bytes 393224 | tf_op jit(solution)/shard_map/ppermute | solution.py:349
  6.5 2.9 %collective-permute-start.2 = (f32[128,256]{1,0:T(8,128)S(1)}, f32[128,256]{1,0:T(8,128)S(1)}, u32[]{:S(2)}, u32[]{:S(2)}) collective-permute-start(f32[128,256]{1,0:T(8,128)S(1)} %get-tuple-element.19), channel_id=1, source_target_pairs={{0,16},{16,0},{1,17},{17,1},{2,18},{18,2},{3,19},{19,3},{4,20},{20... | collective-permute-start | bytes 393224 | tf_op jit(solution)/shard_map/ppermute | solution.py:349
  9.3 1.3 %collective-permute-start.3 = (f32[64,128]{1,0:T(8,128)S(1)}, f32[64,128]{1,0:T(8,128)S(1)}, u32[]{:S(2)}, u32[]{:S(2)}) collective-permute-start(f32[64,128]{1,0:T(8,128)S(1)} %pad_maximum_fusion.3), channel_id=1, source_target_pairs={{0,16},{16,0},{1,17},{17,1},{2,18},{18,2},{3,19},{19,3},{4,20},{20... | collective-permute-start | bytes 98312 | tf_op jit(solution)/shard_map/ppermute | solution.py:349
  10.6 0.7 copy-start.8
  11.3 1.0 %copy-start.2 = (f32[2,256,256]{2,1,0:T(8,128)S(1)}, f32[2,256,256]{2,1,0:T(8,128)}, u32[]{:S(2)}) copy-start(f32[2,256,256]{2,1,0:T(8,128)} %probe.1) | copy-start | bytes 1572868
  12.3 1.2 %copy-start.6 = (bf16[8,256,256]{2,1,0:T(8,128)(2,1)S(1)}, bf16[8,256,256]{2,1,0:T(8,128)(2,1)}, u32[]{:S(2)}) copy-start(bf16[8,256,256]{2,1,0:T(8,128)(2,1)} %constant.55.clone.rest_4_) | copy-start | bytes 3145732
  13.6 1.0 %copy-start.7 = (f32[1,1,2,256,256]{4,3,2,1,0:T(8,128)S(1)}, f32[1,1,2,256,256]{4,3,2,1,0:T(8,128)}, u32[]{:S(2)}) copy-start(f32[1,1,2,256,256]{4,3,2,1,0:T(8,128)} %param.8) | copy-start | bytes 1572868
  23.9 1.8 %collective-permute-start.4 = (f32[416,256]{1,0:T(8,128)S(1)}, f32[416,256]{1,0:T(8,128)S(1)}, u32[]{:S(2)}, u32[]{:S(2)}) collective-permute-start(f32[416,256]{1,0:T(8,128)S(1)} %get-tuple-element.24), channel_id=1, source_target_pairs={{0,16},{16,0},{1,17},{17,1},{2,18},{18,2},{3,19},{19,3},{4,20},{20... | collective-permute-start | bytes 1277960 | tf_op jit(solution)/shard_map/ppermute | solution.py:349
  26.4 14.2 %collective-permute-start.5 = (f32[256,256]{1,0:T(8,128)S(1)}, f32[256,256]{1,0:T(8,128)S(1)}, u32[]{:S(2)}, u32[]{:S(2)}) collective-permute-start(f32[256,256]{1,0:T(8,128)S(1)} %get-tuple-element.26), channel_id=1, source_target_pairs={{0,1},{1,0},{2,3},{3,2},{4,5},{5,4},{6,7},{7,6},{8,9},{9,8},{10,11... | collective-permute-start | bytes 786440 | tf_op jit(solution)/shard_map/ppermute | solution.py:349
  31.8 8.9 %collective-permute-start.7 = (f32[128,256]{1,0:T(8,128)S(1)}, f32[128,256]{1,0:T(8,128)S(1)}, u32[]{:S(2)}, u32[]{:S(2)}) collective-permute-start(f32[128,256]{1,0:T(8,128)S(1)} %get-tuple-element.27), channel_id=1, source_target_pairs={{1,2},{2,1},{3,4},{4,3},{5,6},{6,5},{7,8},{8,7},{9,10},{10,9},{11,... | collective-permute-start | bytes 393224 | tf_op jit(solution)/shard_map/ppermute | solution.py:349
  40.6 4.3 %collective-permute-start.6 = (f32[64,256]{1,0:T(8,128)S(1)}, f32[64,256]{1,0:T(8,128)S(1)}, u32[]{:S(2)}, u32[]{:S(2)}) collective-permute-start(f32[64,256]{1,0:T(8,128)S(1)} %get-tuple-element.36), channel_id=1, source_target_pairs={{0,2},{1,3},{2,0},{3,1},{4,6},{5,7},{6,4},{7,5},{8,10},{9,11},{10,... | collective-permute-start | bytes 196616 | tf_op jit(solution)/shard_map/ppermute | solution.py:341
  45.9 1.0 %copy-start.4 = (f32[4,256,256]{2,1,0:T(8,128)}, f32[4,256,256]{2,1,0:T(8,128)S(1)}, u32[]{:S(2)}) copy-start(f32[4,256,256]{2,1,0:T(8,128)S(1)} %get-tuple-element.28.descent) | copy-start | bytes 3145732
  46.9 4.6 %collective-permute-start.8 = (f32[72,256]{1,0:T(8,128)S(1)}, f32[72,256]{1,0:T(8,128)S(1)}, u32[]{:S(2)}, u32[]{:S(2)}) collective-permute-start(f32[72,256]{1,0:T(8,128)S(1)} %get-tuple-element.29), channel_id=1, source_target_pairs={{0,4},{1,5},{2,6},{3,7},{4,0},{5,1},{6,2},{7,3},{8,12},{9,13},{10,... | collective-permute-start | bytes 221192 | tf_op jit(solution)/shard_map/ppermute | solution.py:341
  49.1 19.6 %copy-start.5 = (f32[4,256,256]{2,1,0:T(8,128)S(1)}, f32[4,256,256]{2,1,0:T(8,128)}, u32[]{:S(2)}) copy-start(f32[4,256,256]{2,1,0:T(8,128)} %copy-done.4) | copy-start | bytes 3145732
  51.5 5.6 %collective-permute-start.9 = (f32[72,256]{1,0:T(8,128)S(1)}, f32[72,256]{1,0:T(8,128)S(1)}, u32[]{:S(2)}, u32[]{:S(2)}) collective-permute-start(f32[72,256]{1,0:T(8,128)S(1)} %maximum_select_fusion.1), channel_id=1, source_target_pairs={{0,8},{1,9},{2,10},{3,11},{4,12},{5,13},{6,14},{7,15},{8,0},{9,1},... | collective-permute-start | bytes 221192 | tf_op jit(solution)/shard_map/ppermute | solution.py:341
  57.2 4.7 %collective-permute-start.10 = (f32[72,256]{1,0:T(8,128)S(1)}, f32[72,256]{1,0:T(8,128)S(1)}, u32[]{:S(2)}, u32[]{:S(2)}) collective-permute-start(f32[72,256]{1,0:T(8,128)S(1)} %maximum_select_fusion), channel_id=1, source_target_pairs={{0,2},{1,3},{2,0},{3,1},{4,6},{5,7},{6,4},{7,5},{8,10},{9,11},{10,... | collective-permute-start | bytes 221192 | tf_op jit(solution)/shard_map/ppermute | solution.py:341
  61.9 5.1 %collective-permute-start.11 = (f32[136,256]{1,0:T(8,128)S(1)}, f32[136,256]{1,0:T(8,128)S(1)}, u32[]{:S(2)}, u32[]{:S(2)}) collective-permute-start(f32[136,256]{1,0:T(8,128)S(1)} %pad_maximum_fusion.1), channel_id=1, source_target_pairs={{0,1},{1,0},{2,3},{3,2},{4,5},{5,4},{6,7},{7,6},{8,9},{9,8},{10,11... | collective-permute-start | bytes 417800 | tf_op jit(solution)/shard_map/ppermute | solution.py:341
  67.0 1.7 %copy-start.3 = (f32[2,256,256]{2,1,0:T(8,128)S(1)}, f32[2,256,256]{2,1,0:T(8,128)}, u32[]{:S(2)}) copy-start(f32[2,256,256]{2,1,0:T(8,128)} %probe.1) | copy-start | bytes 1572868
  67.1 1.6 %collective-permute-start.12 = (f32[264,256]{1,0:T(8,128)S(1)}, f32[264,256]{1,0:T(8,128)S(1)}, u32[]{:S(2)}, u32[]{:S(2)}) collective-permute-start(f32[264,256]{1,0:T(8,128)S(1)} %pad_maximum_fusion.mine), channel_id=1, source_target_pairs={{0,16},{16,0},{1,17},{17,1},{2,18},{18,2},{3,19},{19,3},{4,20},{20... | collective-permute-start | bytes 811016 | tf_op jit(solution)/shard_map/ppermute | solution.py:341

commit v2 on v1

--- a/solution.py
+++ b/solution.py
@@ -9,11 +9,13 @@
 from jax.experimental.pallas import tpu as pltpu
 from jax.sharding import PartitionSpec as P
 
+
 RIM = 32
 LANES = 128
 PLANES = 4
 VMEM = pl.BlockSpec(memory_space=pltpu.VMEM)
 SMEM = pl.BlockSpec(memory_space=pltpu.SMEM)
+HBM = pl.BlockSpec(memory_space=pltpu.HBM)
 f32 = jnp.float32
 bf16 = jnp.bfloat16
 
@@ -49,12 +51,17 @@
     return lax.broadcasted_iota(jnp.int32, (rows, LANES), 1)
 
 
-def pack_kernel(par, obj, col1, col2, *row_msgs):
+def pack_kernel(par, obj_hbm, obj, col1, col2, *rest):
+    row_msgs, sem = rest[:-1], rest[-1]
     extent = obj.shape[-1]
     lane = lanes_of(extent)
     left = jnp.zeros((extent, LANES), f32)
     right = jnp.zeros((extent, LANES), f32)
+    copies = [pltpu.make_async_copy(obj_hbm.at[q], obj.at[q], sem.at[q]) for q in range(PLANES)]
+    for copy in copies:
+        copy.start()
     for q in range(PLANES):
+        copies[q].wait()
         inside = (lane >= RIM * q) & (lane < RIM * (q + 1))
         head = obj[q, :, :LANES]
         tail = obj[q, :, extent - LANES :]
@@ -72,22 +79,25 @@
             msg[RIM * q : RIM * (q + 1), :] = obj[q, pl.ds(start, RIM), :]
 
 
-def tile_kernel(sides, pos, par, obj, col1, col2, *rest):
-    row_in = rest[:sides]
-    corner_in = rest[sides : 2 * sides]
-    probe, measured, tabs = rest[2 * sides : 2 * sides + 3]
-    outs = rest[2 * sides + 3 :]
-    row_out = outs[:sides]
-    keep_out, inner_out, left_out, right_out = outs[sides : sides + 4]
-    window, grad, patch, wave, mats, right_in, left_in = outs[sides + 4 :]
+def prep_kernel(par, obj, probe_hbm, measured_hbm, tabs_hbm, probe, measured, mats, window, mask2, mask4, tabs, sem):
     extent = obj.shape[-1]
     tiles = extent // LANES
-    count = pos.shape[0]
-    span = extent + 2 * RIM
-    lane = lanes_of(extent)
-    odd_row = par[0]
-    odd_col = par[1] == 1
-
+    copies = [
+        pltpu.make_async_copy(tabs_hbm, tabs, sem.at[0]),
+        pltpu.make_async_copy(probe_hbm, probe, sem.at[1]),
+        pltpu.make_async_copy(measured_hbm, measured, sem.at[2]),
+    ]
+    for copy in copies:
+        copy.start()
+    for q in range(PLANES):
+        for t in range(tiles + 2):
+            window[q, t, :RIM, :] = jnp.zeros((RIM, LANES), f32)
+            window[q, t, RIM + extent :, :] = jnp.zeros((RIM, LANES), f32)
+        for t in range(tiles):
+            window[q, t + 1, RIM : RIM + extent, :] = obj[q, :, LANES * t : LANES * (t + 1)]
+    mask2[...] = jnp.full(mask2.shape, par[2], jnp.int32).astype(f32)
+    mask4[...] = jnp.full(mask4.shape, par[3], jnp.int32).astype(f32)
+    copies[0].wait()
     for part in range(2):
         a_re, a_im, cosine, sine = (tabs[2 * t + part] for t in range(4))
         for index, diag, upper, lower in (
@@ -100,16 +110,30 @@
             mats[index, part, extent:, extent:] = diag
             mats[index, part, :extent, extent:] = upper
             mats[index, part, extent:, :extent] = lower
+    copies[1].wait()
+    copies[2].wait()
+
+
+def tile_kernel(sides, pos, par, col1, col2, *rest):
+    row_in = rest[:sides]
+    corner_in = rest[sides : 2 * sides]
+    probe, measured, mats, _ = rest[2 * sides : 2 * sides + 4]
+    outs = rest[2 * sides + 4 :]
+    row_out = outs[:sides]
+    keep_out, inner_out, left_out, right_out, window = outs[sides : sides + 5]
+    grad, patch, wave, right_in, left_in = outs[sides + 5 :]
+    extent = probe.shape[-1]
+    tiles = extent // LANES
+    count = pos.shape[0]
+    span = extent + 2 * RIM
+    lane = lanes_of(extent)
+    odd_row = par[0]
+    odd_col = par[1] == 1
 
     rim1 = col1[...]
     rim2 = col2[...]
     from_left = jnp.where(odd_col, rim1, rim2)
     from_right = jnp.where(odd_col, rim2, rim1)
-    if sides == 1:
-        start = pl.multiple_of(odd_row * (extent + RIM), RIM)
-        for q in range(PLANES):
-            for t in range(tiles + 2):
-                window[q, t, pl.ds(start, RIM), :] = jnp.zeros((RIM, LANES), f32)
     starts = [pl.multiple_of((1 - (odd_row + n) % 2) * (extent + RIM), RIM) for n in range(sides)]
     for q in range(PLANES):
         turn_left = (LANES - RIM - RIM * q) % LANES
@@ -117,8 +141,6 @@
         turned = lambda value, turn: pltpu.roll(value, turn, 1) if turn else value
         window[q, 0, RIM : RIM + extent, :] = turned(from_left, turn_left)
         window[q, tiles + 1, RIM : RIM + extent, :] = turned(from_right, turn_right)
-        for t in range(tiles):
-            window[q, t + 1, RIM : RIM + extent, :] = obj[q, :, LANES * t : LANES * (t + 1)]
         for n in range(sides):
             corner1 = corner_in[n][:RIM, :]
             corner2 = corner_in[n][RIM:, :]
@@ -206,7 +228,6 @@
         br, bi = patch[p, 2], patch[p, 3]
         to_right(p, br * hr + bi * hi, br * hi - bi * hr)
     right_stage(1)
-    total_re = total_im = None
     for p in range(count):
         er, ei = left_stage(0, p)
         pr, pi = probe[0], probe[1]
@@ -249,30 +270,45 @@
         row_out[n][at : at + RIM, LANES : 2 * LANES] = packed(tiles + 1, False, starts[n], RIM)
 
 
+def corner_kernel(par, col1, col2, *msgs):
+    extent = col1.shape[0]
+    for n, msg in enumerate(msgs):
+        start = pl.multiple_of((1 - (par[0] + n) % 2) * (extent - RIM), RIM)
+        msg[:RIM, :] = col1[pl.ds(start, RIM), :]
+        msg[RIM:, :] = col2[pl.ds(start, RIM), :]
+
+
+def split_kernel(par, mine, other, keep, send):
+    half = mine.shape[0] // 2
+    kept = pl.multiple_of(par[3] * half, half)
+    sent = pl.multiple_of((1 - par[3]) * half, half)
+    keep[...] = mine[pl.ds(kept, half), :] + other[pl.ds(kept, half), :]
+    send[...] = mine[pl.ds(sent, half), :] + other[pl.ds(sent, half), :]
+
+
 def cols_kernel(sides, par, keep, left, right, *rest):
     row_in = rest[:sides]
-    msg1, msg2, keep2, edge = rest[sides:]
+    probe_msg, probe_keep, msg1, msg2, edge = rest[sides:]
     extent = left.shape[0]
     half = extent // 2
     odd_col = par[1] == 1
+    up = par[2] == 1
+    edge[0] = left[...]
+    edge[1] = right[...]
     for n in range(sides):
         base = (extent if n == 0 else 0) + RIM * PLANES
         start = pl.multiple_of((1 - (par[0] + n) % 2) * (extent - RIM), RIM)
-        if n == 0:
-            edge[0] = left[...]
-            edge[1] = right[...]
         for s in range(2):
             edge[s, pl.ds(start, RIM), :] += row_in[n][base : base + RIM, LANES * s : LANES * (s + 1)]
     to1 = jnp.where(odd_col, edge[0], edge[1])
     to2 = jnp.where(odd_col, edge[1], edge[0])
     lower = keep[:half, :] + row_in[0][:half, :]
     upper = keep[half:, :] + row_in[0][half:extent, :]
-    keep2[...] = jnp.where(odd_col, upper, lower)
-    msg1[:half, :] = jnp.where(odd_col, lower, upper)
-    msg1[half:, :LANES] = to1[:half]
-    msg1[half:, LANES:] = to1[half:]
-    msg2[:, :LANES] = to2[:half]
-    msg2[:, LANES:] = to2[half:]
+    probe_keep[...] = jnp.where(up, upper, lower)
+    probe_msg[...] = jnp.where(up, lower, upper)
+    for msg, value in ((msg1, to1), (msg2, to2)):
+        msg[:, :LANES] = value[:half]
+        msg[:, LANES:] = value[half:]
 
 
 def gather_kernel(sides, par, inner, keep3, got3, col1, col2, *rest):
@@ -281,7 +317,6 @@
     extent = inner.shape[-1]
     half = extent // 2
     quarter = keep3.shape[0]
-    tiles = extent // LANES
     odd_col = par[1] == 1
     lane = lanes_of(half)
     descent[...] = inner[...]
@@ -291,7 +326,7 @@
         for q in range(PLANES):
             descent[q, pl.ds(start, RIM), :] += row_in[n][base + RIM * q : base + RIM * (q + 1), :]
     for s in range(2):
-        rim1 = col1[half:, LANES * s : LANES * (s + 1)]
+        rim1 = col1[:, LANES * s : LANES * (s + 1)]
         rim2 = col2[:, LANES * s : LANES * (s + 1)]
         from_left = jnp.where(odd_col, rim1, rim2)
         from_right = jnp.where(odd_col, rim2, rim1)
@@ -312,28 +347,36 @@
     msg[quarter:, :] = peak
 
 
-def final_kernel(rate, par, obj, descent, probe, mine, other, obj_out, probe_out):
+def final_kernel(rate, par, obj, descent, probe, mine, other, obj_out, probe_out, buf, sem):
     extent = obj.shape[-1]
     odd_row = par[0] == 1
+    sums = (jnp.where(odd_row, other[:extent, :], mine[:extent, :]), jnp.where(odd_row, mine[:extent, :], other[:extent, :]))
+    copies = [pltpu.make_async_copy(buf.at[q], obj_out.at[q], sem.at[q]) for q in range(PLANES)]
+    copies += [pltpu.make_async_copy(buf.at[PLANES + c], probe_out.at[c], sem.at[PLANES + c]) for c in range(2)]
+    for c in range(2):
+        buf[PLANES + c] = probe[c] - rate * sums[c]
+        copies[PLANES + c].start()
     peak = jnp.max(jnp.maximum(mine[extent:, :], other[extent:, :]))
     peak = jnp.broadcast_to(peak, (8, extent))
     scale = (0.3 / (jnp.sqrt(peak) + 1e-06))[:1, :]
     for q in range(PLANES):
-        obj_out[q] = obj[q] - descent[q] * scale
-    probe_out[0] = probe[0] - rate * jnp.where(odd_row, other[:extent, :], mine[:extent, :])
-    probe_out[1] = probe[1] - rate * jnp.where(odd_row, mine[:extent, :], other[:extent, :])
-
-
-def call(kernel, outs, ins, scratch=(), smem=1, name=None):
+        buf[q] = obj[q] - descent[q] * scale
+        copies[q].start()
+    for copy in copies:
+        copy.wait()
+
+
+def call(kernel, outs, ins, scratch=(), smem=1, in_hbm=(), out_hbm=(), alias=None, limit=8):
+    shapes = [out if isinstance(out, jax.ShapeDtypeStruct) else jax.ShapeDtypeStruct(out, f32) for out in outs]
     return pl.pallas_call(
         kernel,
-        out_shape=tuple(jax.ShapeDtypeStruct(shape, f32) for shape in outs),
-        in_specs=[SMEM] * smem + [VMEM] * (len(ins) - smem),
-        out_specs=tuple(VMEM for _ in outs),
+        out_shape=tuple(shapes),
+        in_specs=[SMEM if i < smem else HBM if i in in_hbm else VMEM for i in range(len(ins))],
+        out_specs=tuple(HBM if i in out_hbm else VMEM for i in range(len(outs))),
         scratch_shapes=list(scratch),
-        compiler_params=pltpu.CompilerParams(vmem_limit_bytes=48 * 1024 * 1024),
-        name=name,
-    )(*ins)
+        input_output_aliases=alias or {},
+        compiler_params=pltpu.CompilerParams(vmem_limit_bytes=limit * 1024 * 1024),
+    )(*[pltpu.with_memory_space_constraint(x, pltpu.HBM) if i in in_hbm else x for i, x in enumerate(ins)])
 
 
 def swap(value, axis, bit):
@@ -349,92 +392,109 @@
     return lax.ppermute(value, axis, links)
 
 
-def local(object_in, probe_in, positions, intensity):
+def step(object_in, probe_in, positions, intensity):
     extent = probe_in.shape[-1]
     half, quarter = extent // 2, extent // 4
     rows, cols = lax.axis_size("row"), lax.axis_size("col")
     sides = 1 if rows == 2 else 2
     row, col = lax.axis_index("row"), lax.axis_index("col")
-    par = jnp.stack([row % 2, col % 2]).astype(jnp.int32)
+    par = jnp.stack([row & 1, col & 1, (col >> 1) & 1, (col >> 2) & 1]).astype(jnp.int32)
     offsets = positions.reshape(-1, 2)
     count = offsets.shape[0]
-    measured = intensity.reshape(-1, extent, extent)
-    obj = object_in.reshape(PLANES, extent, extent)
+    measured_in = intensity.reshape(-1, extent, extent)
+    obj_in = object_in.reshape(PLANES, extent, extent)
     tabs = jnp.asarray(tables(extent))
-
-    sent = call(pack_kernel, [(extent, LANES)] * 2 + [(PLANES * RIM, extent)] * sides, (par, obj), name="pack")
+    span = extent + 2 * RIM
+    tiles = extent // LANES
+    rim_rows = RIM * (PLANES + 1)
+
+    obj, *sent = call(
+        pack_kernel,
+        [obj_in.shape] + [(extent, LANES)] * 2 + [(PLANES * RIM, extent)] * sides,
+        (par, obj_in),
+        scratch=[pltpu.SemaphoreType.DMA((PLANES,))],
+        in_hbm=(1,),
+    )
     col2 = pairs(sent[1], "col", 1)
     col1 = pairs(sent[0], "col", 0)
     row_in = [pairs(sent[2 + n], "row", n) for n in range(sides)]
-    corner_in = []
-    for n in range(sides):
-        start = jnp.where((row + n) % 2 == 0, extent - RIM, 0)
-        corner = jnp.concatenate([lax.dynamic_slice_in_dim(c, start, RIM, 0) for c in (col1, col2)], 0)
-        corner_in.append(pairs(corner, "row", n))
-
-    span = extent + 2 * RIM
-    tiles = extent // LANES
-    rim_rows = RIM * (PLANES + 1)
-    wide = (2 * extent, 2 * extent)
+    probe, measured, mats, window, mask2, mask4 = call(
+        prep_kernel,
+        [
+            probe_in.shape,
+            measured_in.shape,
+            jax.ShapeDtypeStruct((4, 2, 2 * extent, 2 * extent), bf16),
+            (PLANES, tiles + 2, span, LANES),
+            (half, extent),
+            (quarter, extent),
+        ],
+        (par, obj, probe_in, measured_in, tabs),
+        scratch=[pltpu.VMEM(tabs.shape, bf16), pltpu.SemaphoreType.DMA((3,))],
+        in_hbm=(2, 3, 4),
+        limit=16,
+    )
+    corners = call(corner_kernel, [(2 * RIM, LANES)] * sides, (par, col1, col2))
+    corner_in = [pairs(corners[n], "row", n) for n in range(sides)]
+
+    ins = (offsets, par, col1, col2, *row_in, *corner_in, probe, measured, mats, window)
+    shapes = [(extent + rim_rows, extent)] + [(rim_rows, extent)] * (sides - 1)
+    shapes += [(extent, extent), (PLANES, extent, extent), (extent, LANES), (extent, LANES), window.shape]
     out = call(
         functools.partial(tile_kernel, sides),
-        [(extent + rim_rows, extent)] + [(rim_rows, extent)] * (sides - 1)
-        + [(extent, extent), (PLANES, extent, extent), (extent, LANES), (extent, LANES)],
-        (offsets, par, obj, col1, col2, *row_in, *corner_in, probe_in, measured, tabs),
+        shapes,
+        ins,
         scratch=[
-            pltpu.VMEM((PLANES, tiles + 2, span, LANES), f32),
             pltpu.VMEM((PLANES, tiles + 2, span, LANES), f32),
             pltpu.VMEM((count, PLANES, extent, extent), f32),
             pltpu.VMEM((count, 2, extent, extent), f32),
-            pltpu.VMEM((4, 2) + wide, bf16),
             pltpu.VMEM((2, count * extent, 2 * extent), bf16),
             pltpu.VMEM((2, 2 * extent, count * extent), bf16),
         ],
         smem=2,
-        name="tile",
+        alias={len(ins) - 1: len(shapes) - 1},
+        limit=32,
     )
     row_back = [pairs(out[n], "row", n) for n in range(sides)]
-    keep, inner, left, right = out[sides:]
-    msg1, msg2, keep2 = call(
+    keep, inner, left, right = out[sides : sides + 4]
+    probe_msg, probe_keep, msg1, msg2 = call(
         functools.partial(cols_kernel, sides),
-        [(extent, extent), (half, extent), (half, extent)],
+        [(half, extent)] * 4,
         (par, keep, left, right, *row_back),
         scratch=[pltpu.VMEM((2, extent, LANES), f32)],
-        name="cols",
-    )
+    )
+    probe_got = swap(probe_msg, "col", 2)
+    got2 = pairs(msg2, "col", 1)
     got1 = pairs(msg1, "col", 0)
-    got2 = pairs(msg2, "col", 1)
-    both = keep2 + got1[:half]
-    up = (col // 2) % 2 == 1
-    keep3 = jnp.where(up, both[quarter:], both[:quarter])
-    got3 = swap(jnp.where(up, both[:quarter], both[quarter:]), "col", 2)
+    keep3, send3 = call(split_kernel, [(quarter, extent)] * 2, (par, probe_keep, probe_got))
+    got3 = swap(send3, "col", 4)
     state, descent = call(
         functools.partial(gather_kernel, sides),
         [(quarter + 8, extent), (PLANES, extent, extent)],
         (par, inner, keep3, got3, got1, got2, *row_back),
-        name="gather",
     )
     is_sum = lax.broadcasted_iota(jnp.int32, state.shape, 0) < quarter
-    steps = [("col", 1 << b) for b in range(2, cols.bit_length() - 1)]
+    steps = [("col", 1 << b) for b in range(3, cols.bit_length() - 1)] + [("col", 1)]
     steps += [("row", 1 << b) for b in range(1, rows.bit_length() - 1)]
     for axis, bit in steps:
         other = swap(state, axis, bit)
         state = jnp.where(is_sum, state + other, jnp.maximum(state, other))
 
-    def joined(state, other, up):
+    def joined(state, other, mask):
         top = state.shape[0] - 8
+        up = mask > 0.5
         low = jnp.where(up, other[:top], state[:top])
         high = jnp.where(up, state[:top], other[:top])
         return jnp.concatenate([low, high, jnp.maximum(state[top:], other[top:])], 0)
 
-    state = joined(state, swap(state, "col", 2), up)
-    state = joined(state, swap(state, "col", 1), col % 2 == 1)
+    state = joined(state, swap(state, "col", 4), mask4)
+    state = joined(state, swap(state, "col", 2), mask2)
     other = swap(state, "row", 1)
     object_out, probe_out = call(
         functools.partial(final_kernel, 2.0 / (rows * cols)),
         [obj.shape, probe_in.shape],
-        (par, obj, descent, probe_in, state, other),
-        name="final",
+        (par, obj, descent, probe, state, other),
+        scratch=[pltpu.VMEM((PLANES + 2, extent, extent), f32), pltpu.SemaphoreType.DMA((PLANES + 2,))],
+        out_hbm=(0, 1),
     )
     return object_out.reshape(object_in.shape), probe_out
 
@@ -447,7 +507,7 @@
         P("row", "col", None, None, None),
     )
     return jax.shard_map(
-        local,
+        step,
         mesh=mesh,
         in_specs=placed,
         out_specs=(P(None, None, "row", "col"), P()),

time: 71.1 us -> 64.8 us (0.911)
  local copies, waits for them, and re-layouts: 6.19 us -> 0.01 us
  waiting for transfers between devices: 29.7 us -> 23.8 us
  Pallas kernels: 13.7 us -> 18.1 us
  starting transfers between devices: 20 us -> 21.5 us
    ppermute x7, waiting for transfers between devices: 13.7 us -> 4.16 us  [pairs(): return lax.ppermute(value, axis, links)]
    unnamed x18 -> x2, local copies, waits for them, and re-layouts: 6.18 us -> 0.01 us
    ppermute x6 -> x7, starting transfers between devices: 9.84 us -> 15 us  [swap(): return lax.ppermute(value, axis, [(i, i ^ bit) for i in range(count)])]
    pallas_call x5 -> x8, Pallas kernels: 13.7 us -> 18.1 us  [call(): pl.pallas_call(kernel, out_shape=tuple(shapes), in_specs=[SMEM if i < sme...]
    ppermute x7, starting transfers between devices: 10.1 us -> 6.47 us  [pairs(): return lax.ppermute(value, axis, links)]
    ppermute x6 -> x7, waiting for transfers between devices: 16 us -> 19.7 us  [swap(): return lax.ppermute(value, axis, [(i, i ^ bit) for i in range(count)])]
  transfers between devices with their start and end apart: 13 -> 14, of which waited for: 10 -> 9; matrix products, arithmetic and copies ran while one was open for 0% -> 0% of each run, Pallas kernels for 0% -> 5%
where the time goes in v2:
time: 64.8 us; the launch traced here: 64.6 us
  waiting for transfers between devices  23.8 us (37%)
  starting transfers between devices  21.5 us (33%)
  Pallas kernels  18.1 us (28%)
  between operations  0.81 us (1%)
    ppermute x7, waiting for transfers between devices, swap(): return lax.ppermute(value, axis, [(i, i ^ bit) for i in range(count)])  19.7 us
    pallas_call x8, Pallas kernels, call(): pl.pallas_call(kernel, out_shape=tuple(shapes), in_specs=[SMEM if i < sme...  18.1 us
    ppermute x7, starting transfers between devices, swap(): return lax.ppermute(value, axis, [(i, i ^ bit) for i in range(count)])  15 us
    ppermute x7, starting transfers between devices, pairs(): return lax.ppermute(value, axis, links)  6.47 us
    ppermute x7, waiting for transfers between devices, pairs(): return lax.ppermute(value, axis, links)  4.16 us
  transfers between devices with their start and end apart: 14, of which 9 were waited for; matrix products, arithmetic and copies ran while one was open for 0% of the time, Pallas kernels for 5%

profile of v2, /device:TPU:0, one launch (start us, length us, event | category | flops | bytes accessed | tf_op | source)
XLA Modules:
  0.0 64.6 jit_solution(7649369810359157731)
XLA Ops:
  0.6 0.0 copy-start
  0.6 0.1 pad_add_fusion.par
  0.7 2.0 %shard_map.68 = (f32[4,256,256]{2,1,0:T(8,128)S(1)}, f32[256,128]{1,0:T(8,128)S(1)}, f32[256,128]{1,0:T(8,128)S(1)}, f32[128,256]{1,0:T(8,128)S(1)}) custom-call(s32[4]{0:T(128)S(1)} %pad_add_fusion.par, f32[4,256,256]{2,1,0:T(8,128)} %bitcast.9), custom_call_target="tpu_custom_call" | custom-call | tf_op jit(solution)/shard_map/pallas_call | solution.py:371
  2.7 3.0 %collective-permute-start = (f32[256,128]{1,0:T(8,128)S(1)}, f32[256,128]{1,0:T(8,128)S(1)}, u32[]{:S(2)}, u32[]{:S(2)}) collective-permute-start(f32[256,128]{1,0:T(8,128)S(1)} %get-tuple-element.28), channel_id=1, source_target_pairs={{0,1},{1,0},{2,3},{3,2},{4,5},{5,4},{6,7},{7,6},{8,9},{9,8},{10,11... | collective-permute-start | bytes 393224 | tf_op jit(solution)/shard_map/ppermute | solution.py:392
  5.8 0.7 %collective-permute-start.1 = (f32[256,128]{1,0:T(8,128)S(1)}, f32[256,128]{1,0:T(8,128)S(1)}, u32[]{:S(2)}, u32[]{:S(2)}) collective-permute-start(f32[256,128]{1,0:T(8,128)S(1)} %get-tuple-element.29), channel_id=1, source_target_pairs={{1,2},{2,1},{3,4},{4,3},{5,6},{6,5},{7,8},{8,7},{9,10},{10,9},{11,... | collective-permute-start | bytes 393224 | tf_op jit(solution)/shard_map/ppermute | solution.py:392
  6.4 0.1 collective-permute-start.2
  6.5 2.8 %collective-permute-done.col1 = f32[256,128]{1,0:T(8,128)S(1)} collective-permute-done((f32[256,128]{1,0:T(8,128)S(1)}, f32[256,128]{1,0:T(8,128)S(1)}, u32[]{:S(2)}, u32[]{:S(2)}) %collective-permute-start) | collective-permute-done | bytes 131104 | tf_op jit(solution)/shard_map/ppermute | solution.py:392
  9.3 0.0 collective-permute-done.1.col2
  9.3 0.6 shard_map.69
  9.8 0.1 collective-permute-start.3
  9.9 2.1 %shard_map.70 = (f32[2,256,256]{2,1,0:T(8,128)S(1)}, f32[2,256,256]{2,1,0:T(8,128)S(1)}, bf16[4,2,512,512]{3,2,1,0:T(8,128)(2,1)S(1)}, f32[4,4,320,128]{3,2,1,0:...) custom-call(s32[4]{0:T(128)S(1)} %pad_add_fusion.par, f32[4,256,256]{2,1,0:T(8,128)S(1)} %get-tuple-element.27.obj, ...), custom_call_target="tpu_custom_call" | custom-call | tf_op jit(solution)/shard_map/pallas_call | solution.py:371
  12.0 0.0 collective-permute-done.2.rest_0_
  12.0 0.0 collective-permute-done.3.rest_1_
  12.0 0.0 copy-done
  12.0 9.6 %shard_map.71 = (f32[416,256]{1,0:T(8,128)S(1)}, f32[256,256]{1,0:T(8,128)S(1)}, f32[4,256,256]{2,1,0:T(8,128)S(1)}, f32[256,128]{1,0:T(8,128)S(1)}, f32[256,128...) custom-call(s32[2,2]{1,0:T(2,128)S(1)} %bitcast.8, s32[4]{0:T(128)S(1)} %pad_add_fusion.par, ...), custom_call_target="tpu_custom_call", output_to_operand_aliasing={{5}: (9, {})} | custom-call | tf_op jit(solution)/shard_map/pallas_call | solution.py:371
  21.6 0.6 collective-permute-start.4
  22.2 1.4 %collective-permute-done.4.rest_0_ = f32[416,256]{1,0:T(8,128)S(1)} collective-permute-done((f32[416,256]{1,0:T(8,128)S(1)}, f32[416,256]{1,0:T(8,128)S(1)}, u32[]{:S(2)}, u32[]{:S(2)}) %collective-permute-start.4) | collective-permute-done | bytes 426016 | tf_op jit(solution)/shard_map/ppermute | solution.py:392
  23.6 0.6 shard_map.72
  24.2 5.9 %collective-permute-start.5 = (f32[128,256]{1,0:T(8,128)S(1)}, f32[128,256]{1,0:T(8,128)S(1)}, u32[]{:S(2)}, u32[]{:S(2)}) collective-permute-start(f32[128,256]{1,0:T(8,128)S(1)} %get-tuple-element.41), channel_id=1, source_target_pairs={{0,2},{1,3},{2,0},{3,1},{4,6},{5,7},{6,4},{7,5},{8,10},{9,11},{10,... | collective-permute-start | bytes 393224 | tf_op jit(solution)/shard_map/ppermute | solution.py:384
  30.1 1.4 %collective-permute-start.7 = (f32[128,256]{1,0:T(8,128)S(1)}, f32[128,256]{1,0:T(8,128)S(1)}, u32[]{:S(2)}, u32[]{:S(2)}) collective-permute-start(f32[128,256]{1,0:T(8,128)S(1)} %get-tuple-element.44), channel_id=1, source_target_pairs={{0,1},{1,0},{2,3},{3,2},{4,5},{5,4},{6,7},{7,6},{8,9},{9,8},{10,11... | collective-permute-start | bytes 393224 | tf_op jit(solution)/shard_map/ppermute | solution.py:392
  31.5 0.7 %collective-permute-start.8 = (f32[128,256]{1,0:T(8,128)S(1)}, f32[128,256]{1,0:T(8,128)S(1)}, u32[]{:S(2)}, u32[]{:S(2)}) collective-permute-start(f32[128,256]{1,0:T(8,128)S(1)} %get-tuple-element.45), channel_id=1, source_target_pairs={{1,2},{2,1},{3,4},{4,3},{5,6},{6,5},{7,8},{8,7},{9,10},{10,9},{11,... | collective-permute-start | bytes 393224 | tf_op jit(solution)/shard_map/ppermute | solution.py:392
  32.1 1.9 %collective-permute-done.5.other = f32[128,256]{1,0:T(8,128)S(1)} collective-permute-done((f32[128,256]{1,0:T(8,128)S(1)}, f32[128,256]{1,0:T(8,128)S(1)}, u32[]{:S(2)}, u32[]{:S(2)}) %collective-permute-start.5) | collective-permute-done | bytes 131104 | tf_op jit(solution)/shard_map/ppermute | solution.py:384
  34.1 0.6 shard_map.73
  34.7 2.7 %collective-permute-start.6 = (f32[64,256]{1,0:T(8,128)S(1)}, f32[64,256]{1,0:T(8,128)S(1)}, u32[]{:S(2)}, u32[]{:S(2)}) collective-permute-start(f32[64,256]{1,0:T(8,128)S(1)} %get-tuple-element.43), channel_id=1, source_target_pairs={{0,4},{1,5},{2,6},{3,7},{4,0},{5,1},{6,2},{7,3},{8,12},{9,13},{10,... | collective-permute-start | bytes 196616 | tf_op jit(solution)/shard_map/ppermute | solution.py:384
  37.4 0.0 collective-permute-done.7.col1
  37.4 0.0 collective-permute-done.8.col2
  37.4 2.4 %collective-permute-done.6.got3 = f32[64,256]{1,0:T(8,128)S(1)} collective-permute-done((f32[64,256]{1,0:T(8,128)S(1)}, f32[64,256]{1,0:T(8,128)S(1)}, u32[]{:S(2)}, u32[]{:S(2)}) %collective-permute-start.6) | collective-permute-done | bytes 65568 | tf_op jit(solution)/shard_map/ppermute | solution.py:384
  39.8 0.9 %shard_map.74 = (f32[72,256]{1,0:T(8,128)S(1)}, f32[4,256,256]{2,1,0:T(8,128)S(1)}) custom-call(s32[4]{0:T(128)S(1)} %pad_add_fusion.par, f32[4,256,256]{2,1,0:T(8,128)S(1)} %get-tuple-element.35.inner, f32[64,256]{1,0:T(8,128)S(1)} %get-tuple-element.42.keep3, f32[64,256]{1,0:T(8,128)S(1)} %collective-permute-done.6.got3, ...), custom_call_target="tpu_custom_call" | custom-call | tf_op jit(solution)/shard_map/pallas_call | solution.py:371
  40.7 3.7 %collective-permute-start.9 = (f32[72,256]{1,0:T(8,128)S(1)}, f32[72,256]{1,0:T(8,128)S(1)}, u32[]{:S(2)}, u32[]{:S(2)}) collective-permute-start(f32[72,256]{1,0:T(8,128)S(1)} %get-tuple-element.49), channel_id=1, source_target_pairs={{0,8},{1,9},{2,10},{3,11},{4,12},{5,13},{6,14},{7,15},{8,0},{9,1},... | collective-permute-start | bytes 221192 | tf_op jit(solution)/shard_map/ppermute | solution.py:384
  44.4 2.3 %collective-permute-done.9 = f32[72,256]{1,0:T(8,128)S(1)} collective-permute-done((f32[72,256]{1,0:T(8,128)S(1)}, f32[72,256]{1,0:T(8,128)S(1)}, u32[]{:S(2)}, u32[]{:S(2)}) %collective-permute-start.9) | collective-permute-done | bytes 73760 | tf_op jit(solution)/shard_map/ppermute | solution.py:384
  46.7 0.1 maximum_select_fusion.1
  46.8 0.1 collective-permute-start.10
  46.9 4.3 %collective-permute-done.10 = f32[72,256]{1,0:T(8,128)S(1)} collective-permute-done((f32[72,256]{1,0:T(8,128)S(1)}, f32[72,256]{1,0:T(8,128)S(1)}, u32[]{:S(2)}, u32[]{:S(2)}) %collective-permute-start.10) | collective-permute-done | bytes 73760 | tf_op jit(solution)/shard_map/ppermute | solution.py:384
  51.2 0.1 maximum_select_fusion
  51.3 2.2 %collective-permute-start.11 = (f32[72,256]{1,0:T(8,128)S(1)}, f32[72,256]{1,0:T(8,128)S(1)}, u32[]{:S(2)}, u32[]{:S(2)}) collective-permute-start(f32[72,256]{1,0:T(8,128)S(1)} %maximum_select_fusion), channel_id=1, source_target_pairs={{0,4},{1,5},{2,6},{3,7},{4,0},{5,1},{6,2},{7,3},{8,12},{9,13},{10,... | collective-permute-start | bytes 221192 | tf_op jit(solution)/shard_map/ppermute | solution.py:384
  53.5 2.3 %collective-permute-done.11 = f32[72,256]{1,0:T(8,128)S(1)} collective-permute-done((f32[72,256]{1,0:T(8,128)S(1)}, f32[72,256]{1,0:T(8,128)S(1)}, u32[]{:S(2)}, u32[]{:S(2)}) %collective-permute-start.11) | collective-permute-done | bytes 73760 | tf_op jit(solution)/shard_map/ppermute | solution.py:384
  55.9 0.4 collective-permute-start.12
  56.3 4.7 %collective-permute-done.12 = f32[136,256]{1,0:T(8,128)S(1)} collective-permute-done((f32[136,256]{1,0:T(8,128)S(1)}, f32[136,256]{1,0:T(8,128)S(1)}, u32[]{:S(2)}, u32[]{:S(2)}) %collective-permute-start.12) | collective-permute-done | bytes 139296 | tf_op jit(solution)/shard_map/ppermute | solution.py:384
  61.1 0.1 collective-permute-start.13
  61.2 1.5 %collective-permute-done.13.other = f32[264,256]{1,0:T(8,128)S(1)} collective-permute-done((f32[264,256]{1,0:T(8,128)S(1)}, f32[264,256]{1,0:T(8,128)S(1)}, u32[]{:S(2)}, u32[]{:S(2)}) %collective-permute-start.13) | collective-permute-done | bytes 270368 | tf_op jit(solution)/shard_map/ppermute | solution.py:384
  62.8 1.8 %shard_map.75 = (f32[4,256,256]{2,1,0:T(8,128)}, f32[2,256,256]{2,1,0:T(8,128)}) custom-call(s32[4]{0:T(128)S(1)} %pad_add_fusion.par, f32[4,256,256]{2,1,0:T(8,128)S(1)} %get-tuple-element.27.obj, f32[4,256,256]{2,1,0:T(8,128)S(1)} %get-tuple-element.46.descent, f32[2,256,256]{2,1,0:T(8,128)S(1)} %get-tuple-element.31.rest_2_.probe, ...), custom_call_target="tpu_custom_call" | custom-call | tf_op jit(solution)/shard_map/pallas_call | solution.py:371
  (9 shorter events, 0.1 us)
Async XLA Ops:
  0.6 11.4 %copy-start = (s32[1,1,2,2]{3,2,1,0:T(2,128)S(1)}, s32[1,1,2,2]{3,2,1,0:T(2,128)}, u32[]{:S(2)}) copy-start(s32[1,1,2,2]{3,2,1,0:T(2,128)} %param.7) | copy-start | bytes 52
  2.7 6.5 %collective-permute-start = (f32[256,128]{1,0:T(8,128)S(1)}, f32[256,128]{1,0:T(8,128)S(1)}, u32[]{:S(2)}, u32[]{:S(2)}) collective-permute-start(f32[256,128]{1,0:T(8,128)S(1)} %get-tuple-element.28), channel_id=1, source_target_pairs={{0,1},{1,0},{2,3},{3,2},{4,5},{5,4},{6,7},{7,6},{8,9},{9,8},{10,11... | collective-permute-start | bytes 393224 | tf_op jit(solution)/shard_map/ppermute | solution.py:392
  5.8 3.5 %collective-permute-start.1 = (f32[256,128]{1,0:T(8,128)S(1)}, f32[256,128]{1,0:T(8,128)S(1)}, u32[]{:S(2)}, u32[]{:S(2)}) collective-permute-start(f32[256,128]{1,0:T(8,128)S(1)} %get-tuple-element.29), channel_id=1, source_target_pairs={{1,2},{2,1},{3,4},{4,3},{5,6},{6,5},{7,8},{8,7},{9,10},{10,9},{11,... | collective-permute-start | bytes 393224 | tf_op jit(solution)/shard_map/ppermute | solution.py:392
  6.4 5.6 %collective-permute-start.2 = (f32[128,256]{1,0:T(8,128)S(1)}, f32[128,256]{1,0:T(8,128)S(1)}, u32[]{:S(2)}, u32[]{:S(2)}) collective-permute-start(f32[128,256]{1,0:T(8,128)S(1)} %get-tuple-element.30), channel_id=1, source_target_pairs={{0,16},{16,0},{1,17},{17,1},{2,18},{18,2},{3,19},{19,3},{4,20},{20... | collective-permute-start | bytes 393224 | tf_op jit(solution)/shard_map/ppermute | solution.py:392
  9.8 2.2 %collective-permute-start.3 = (f32[64,128]{1,0:T(8,128)S(1)}, f32[64,128]{1,0:T(8,128)S(1)}, u32[]{:S(2)}, u32[]{:S(2)}) collective-permute-start(f32[64,128]{1,0:T(8,128)S(1)} %shard_map.69), channel_id=1, source_target_pairs={{0,16},{16,0},{1,17},{17,1},{2,18},{18,2},{3,19},{19,3},{4,20},{20... | collective-permute-start | bytes 98312 | tf_op jit(solution)/shard_map/ppermute | solution.py:392
  21.6 2.0 %collective-permute-start.4 = (f32[416,256]{1,0:T(8,128)S(1)}, f32[416,256]{1,0:T(8,128)S(1)}, u32[]{:S(2)}, u32[]{:S(2)}) collective-permute-start(f32[416,256]{1,0:T(8,128)S(1)} %get-tuple-element.39), channel_id=1, source_target_pairs={{0,16},{16,0},{1,17},{17,1},{2,18},{18,2},{3,19},{19,3},{4,20},{20... | collective-permute-start | bytes 1277960 | tf_op jit(solution)/shard_map/ppermute | solution.py:392
  24.2 9.9 %collective-permute-start.5 = (f32[128,256]{1,0:T(8,128)S(1)}, f32[128,256]{1,0:T(8,128)S(1)}, u32[]{:S(2)}, u32[]{:S(2)}) collective-permute-start(f32[128,256]{1,0:T(8,128)S(1)} %get-tuple-element.41), channel_id=1, source_target_pairs={{0,2},{1,3},{2,0},{3,1},{4,6},{5,7},{6,4},{7,5},{8,10},{9,11},{10,... | collective-permute-start | bytes 393224 | tf_op jit(solution)/shard_map/ppermute | solution.py:384
  30.1 7.3 %collective-permute-start.7 = (f32[128,256]{1,0:T(8,128)S(1)}, f32[128,256]{1,0:T(8,128)S(1)}, u32[]{:S(2)}, u32[]{:S(2)}) collective-permute-start(f32[128,256]{1,0:T(8,128)S(1)} %get-tuple-element.44), channel_id=1, source_target_pairs={{0,1},{1,0},{2,3},{3,2},{4,5},{5,4},{6,7},{7,6},{8,9},{9,8},{10,11... | collective-permute-start | bytes 393224 | tf_op jit(solution)/shard_map/ppermute | solution.py:392
  31.5 5.9 %collective-permute-start.8 = (f32[128,256]{1,0:T(8,128)S(1)}, f32[128,256]{1,0:T(8,128)S(1)}, u32[]{:S(2)}, u32[]{:S(2)}) collective-permute-start(f32[128,256]{1,0:T(8,128)S(1)} %get-tuple-element.45), channel_id=1, source_target_pairs={{1,2},{2,1},{3,4},{4,3},{5,6},{6,5},{7,8},{8,7},{9,10},{10,9},{11,... | collective-permute-start | bytes 393224 | tf_op jit(solution)/shard_map/ppermute | solution.py:392
  34.7 5.2 %collective-permute-start.6 = (f32[64,256]{1,0:T(8,128)S(1)}, f32[64,256]{1,0:T(8,128)S(1)}, u32[]{:S(2)}, u32[]{:S(2)}) collective-permute-start(f32[64,256]{1,0:T(8,128)S(1)} %get-tuple-element.43), channel_id=1, source_target_pairs={{0,4},{1,5},{2,6},{3,7},{4,0},{5,1},{6,2},{7,3},{8,12},{9,13},{10,... | collective-permute-start | bytes 196616 | tf_op jit(solution)/shard_map/ppermute | solution.py:384
  40.7 6.0 %collective-permute-start.9 = (f32[72,256]{1,0:T(8,128)S(1)}, f32[72,256]{1,0:T(8,128)S(1)}, u32[]{:S(2)}, u32[]{:S(2)}) collective-permute-start(f32[72,256]{1,0:T(8,128)S(1)} %get-tuple-element.49), channel_id=1, source_target_pairs={{0,8},{1,9},{2,10},{3,11},{4,12},{5,13},{6,14},{7,15},{8,0},{9,1},... | collective-permute-start | bytes 221192 | tf_op jit(solution)/shard_map/ppermute | solution.py:384
  46.8 4.4 %collective-permute-start.10 = (f32[72,256]{1,0:T(8,128)S(1)}, f32[72,256]{1,0:T(8,128)S(1)}, u32[]{:S(2)}, u32[]{:S(2)}) collective-permute-start(f32[72,256]{1,0:T(8,128)S(1)} %maximum_select_fusion.1), channel_id=1, source_target_pairs={{0,1},{1,0},{2,3},{3,2},{4,5},{5,4},{6,7},{7,6},{8,9},{9,8},{10,11... | collective-permute-start | bytes 221192 | tf_op jit(solution)/shard_map/ppermute | solution.py:384
  51.3 4.5 %collective-permute-start.11 = (f32[72,256]{1,0:T(8,128)S(1)}, f32[72,256]{1,0:T(8,128)S(1)}, u32[]{:S(2)}, u32[]{:S(2)}) collective-permute-start(f32[72,256]{1,0:T(8,128)S(1)} %maximum_select_fusion), channel_id=1, source_target_pairs={{0,4},{1,5},{2,6},{3,7},{4,0},{5,1},{6,2},{7,3},{8,12},{9,13},{10,... | collective-permute-start | bytes 221192 | tf_op jit(solution)/shard_map/ppermute | solution.py:384
  55.9 5.1 %collective-permute-start.12 = (f32[136,256]{1,0:T(8,128)S(1)}, f32[136,256]{1,0:T(8,128)S(1)}, u32[]{:S(2)}, u32[]{:S(2)}) collective-permute-start(f32[136,256]{1,0:T(8,128)S(1)} %pad_maximum_fusion.1), channel_id=1, source_target_pairs={{0,2},{1,3},{2,0},{3,1},{4,6},{5,7},{6,4},{7,5},{8,10},{9,11},{10,... | collective-permute-start | bytes 417800 | tf_op jit(solution)/shard_map/ppermute | solution.py:384
  61.1 1.6 %collective-permute-start.13 = (f32[264,256]{1,0:T(8,128)S(1)}, f32[264,256]{1,0:T(8,128)S(1)}, u32[]{:S(2)}, u32[]{:S(2)}) collective-permute-start(f32[264,256]{1,0:T(8,128)S(1)} %pad_maximum_fusion.mine), channel_id=1, source_target_pairs={{0,16},{16,0},{1,17},{17,1},{2,18},{18,2},{3,19},{19,3},{4,20},{20... | collective-permute-start | bytes 811016 | tf_op jit(solution)/shard_map/ppermute | solution.py:384

commit v3 on v2

--- a/solution.py
+++ b/solution.py
@@ -14,7 +14,6 @@
 LANES = 128
 PLANES = 4
 VMEM = pl.BlockSpec(memory_space=pltpu.VMEM)
-SMEM = pl.BlockSpec(memory_space=pltpu.SMEM)
 HBM = pl.BlockSpec(memory_space=pltpu.HBM)
 f32 = jnp.float32
 bf16 = jnp.bfloat16
@@ -51,8 +50,14 @@
     return lax.broadcasted_iota(jnp.int32, (rows, LANES), 1)
 
 
-def pack_kernel(par, obj_hbm, obj, col1, col2, *rest):
+def parities():
+    row, col = lax.axis_index("row"), lax.axis_index("col")
+    return row & 1, col & 1, (col >> 1) & 1, (col >> 2) & 1
+
+
+def pack_kernel(obj_hbm, obj, col1, col2, *rest):
     row_msgs, sem = rest[:-1], rest[-1]
+    par = parities()
     extent = obj.shape[-1]
     lane = lanes_of(extent)
     left = jnp.zeros((extent, LANES), f32)
@@ -79,9 +84,10 @@
             msg[RIM * q : RIM * (q + 1), :] = obj[q, pl.ds(start, RIM), :]
 
 
-def prep_kernel(par, obj, probe_hbm, measured_hbm, tabs_hbm, probe, measured, mats, window, mask2, mask4, tabs, sem):
+def prep_kernel(obj, probe_hbm, measured_hbm, tabs_hbm, probe, measured, mats, window, grad, mask2, mask4, tabs, sem):
     extent = obj.shape[-1]
     tiles = extent // LANES
+    par = parities()
     copies = [
         pltpu.make_async_copy(tabs_hbm, tabs, sem.at[0]),
         pltpu.make_async_copy(probe_hbm, probe, sem.at[1]),
@@ -91,6 +97,7 @@
         copy.start()
     for q in range(PLANES):
         for t in range(tiles + 2):
+            grad[q, t] = jnp.zeros(grad.shape[2:], f32)
             window[q, t, :RIM, :] = jnp.zeros((RIM, LANES), f32)
             window[q, t, RIM + extent :, :] = jnp.zeros((RIM, LANES), f32)
         for t in range(tiles):
@@ -114,18 +121,20 @@
     copies[2].wait()
 
 
-def tile_kernel(sides, pos, par, col1, col2, *rest):
+def tile_kernel(sides, pos_hbm, col1, col2, *rest):
     row_in = rest[:sides]
     corner_in = rest[sides : 2 * sides]
-    probe, measured, mats, _ = rest[2 * sides : 2 * sides + 4]
-    outs = rest[2 * sides + 4 :]
+    probe, measured, mats = rest[2 * sides : 2 * sides + 3]
+    outs = rest[2 * sides + 5 :]
     row_out = outs[:sides]
-    keep_out, inner_out, left_out, right_out, window = outs[sides : sides + 5]
-    grad, patch, wave, right_in, left_in = outs[sides + 5 :]
+    keep_out, inner_out, left_out, right_out, window, grad = outs[sides : sides + 6]
+    patch, wave, right_in, left_in, pos, sem = outs[sides + 6 :]
+    fetch = pltpu.make_async_copy(pos_hbm, pos, sem)
+    fetch.start()
+    par = parities()
     extent = probe.shape[-1]
     tiles = extent // LANES
     count = pos.shape[0]
-    span = extent + 2 * RIM
     lane = lanes_of(extent)
     odd_row = par[0]
     odd_col = par[1] == 1
@@ -149,9 +158,7 @@
             for t in range(tiles):
                 window[q, t + 1, pl.ds(starts[n], RIM), :] = row_in[n][RIM * q : RIM * (q + 1), LANES * t : LANES * (t + 1)]
 
-    for q in range(PLANES):
-        for t in range(tiles + 2):
-            grad[q, t] = jnp.zeros((span, LANES), f32)
+    fetch.wait()
 
     def place(p):
         across = pos[p, 1] + LANES
@@ -167,23 +174,20 @@
             right_in[1, cols(p), cols(c)] = low
 
     def right_stage(index):
-        for p in range(count):
-            for c in range(2):
-                first = jnp.dot(right_in[0, cols(p), :], mats[index, 0, :, cols(c)], preferred_element_type=f32)
-                first += jnp.dot(right_in[0, cols(p), :], mats[index, 1, :, cols(c)], preferred_element_type=f32)
-                first += jnp.dot(right_in[1, cols(p), :], mats[index, 0, :, cols(c)], preferred_element_type=f32)
-                high, low = split(first)
+        for c in range(2):
+            both = jnp.dot(right_in[0], mats[index, 0, :, cols(c)], preferred_element_type=f32)
+            both += jnp.dot(right_in[0], mats[index, 1, :, cols(c)], preferred_element_type=f32)
+            both += jnp.dot(right_in[1], mats[index, 0, :, cols(c)], preferred_element_type=f32)
+            for p in range(count):
+                high, low = split(both[cols(p)])
                 left_in[0, cols(c), cols(p)] = high
                 left_in[1, cols(c), cols(p)] = low
 
     def left_stage(index, p):
-        out = []
-        for c in range(2):
-            first = jnp.dot(mats[index, 0, cols(c), :], left_in[0, :, cols(p)], preferred_element_type=f32)
-            first += jnp.dot(mats[index, 1, cols(c), :], left_in[0, :, cols(p)], preferred_element_type=f32)
-            first += jnp.dot(mats[index, 0, cols(c), :], left_in[1, :, cols(p)], preferred_element_type=f32)
-            out.append(first)
-        return out
+        both = jnp.dot(mats[index, 0], left_in[0, :, cols(p)], preferred_element_type=f32)
+        both += jnp.dot(mats[index, 1], left_in[0, :, cols(p)], preferred_element_type=f32)
+        both += jnp.dot(mats[index, 0], left_in[1, :, cols(p)], preferred_element_type=f32)
+        return both[:extent], both[extent:]
 
     def add_piece(p, q, value):
         down, first, turn = place(p)
@@ -270,7 +274,8 @@
         row_out[n][at : at + RIM, LANES : 2 * LANES] = packed(tiles + 1, False, starts[n], RIM)
 
 
-def corner_kernel(par, col1, col2, *msgs):
+def corner_kernel(col1, col2, *msgs):
+    par = parities()
     extent = col1.shape[0]
     for n, msg in enumerate(msgs):
         start = pl.multiple_of((1 - (par[0] + n) % 2) * (extent - RIM), RIM)
@@ -278,7 +283,8 @@
         msg[RIM:, :] = col2[pl.ds(start, RIM), :]
 
 
-def split_kernel(par, mine, other, keep, send):
+def split_kernel(mine, other, keep, send):
+    par = parities()
     half = mine.shape[0] // 2
     kept = pl.multiple_of(par[3] * half, half)
     sent = pl.multiple_of((1 - par[3]) * half, half)
@@ -286,7 +292,8 @@
     send[...] = mine[pl.ds(sent, half), :] + other[pl.ds(sent, half), :]
 
 
-def cols_kernel(sides, par, keep, left, right, *rest):
+def cols_kernel(sides, keep, left, right, *rest):
+    par = parities()
     row_in = rest[:sides]
     probe_msg, probe_keep, msg1, msg2, edge = rest[sides:]
     extent = left.shape[0]
@@ -311,9 +318,10 @@
         msg[:, LANES:] = value[half:]
 
 
-def gather_kernel(sides, par, inner, keep3, got3, col1, col2, *rest):
+def gather_kernel(sides, inner, keep3, got3, col1, col2, *rest):
     row_in = rest[:sides]
     msg, descent = rest[sides:]
+    par = parities()
     extent = inner.shape[-1]
     half = extent // 2
     quarter = keep3.shape[0]
@@ -347,9 +355,9 @@
     msg[quarter:, :] = peak
 
 
-def final_kernel(rate, par, obj, descent, probe, mine, other, obj_out, probe_out, buf, sem):
+def final_kernel(rate, obj, descent, probe, mine, other, obj_out, probe_out, buf, sem):
     extent = obj.shape[-1]
-    odd_row = par[0] == 1
+    odd_row = parities()[0] == 1
     sums = (jnp.where(odd_row, other[:extent, :], mine[:extent, :]), jnp.where(odd_row, mine[:extent, :], other[:extent, :]))
     copies = [pltpu.make_async_copy(buf.at[q], obj_out.at[q], sem.at[q]) for q in range(PLANES)]
     copies += [pltpu.make_async_copy(buf.at[PLANES + c], probe_out.at[c], sem.at[PLANES + c]) for c in range(2)]
@@ -366,12 +374,12 @@
         copy.wait()
 
 
-def call(kernel, outs, ins, scratch=(), smem=1, in_hbm=(), out_hbm=(), alias=None, limit=8):
+def call(kernel, outs, ins, scratch=(), in_hbm=(), out_hbm=(), alias=None, limit=8):
     shapes = [out if isinstance(out, jax.ShapeDtypeStruct) else jax.ShapeDtypeStruct(out, f32) for out in outs]
     return pl.pallas_call(
         kernel,
         out_shape=tuple(shapes),
-        in_specs=[SMEM if i < smem else HBM if i in in_hbm else VMEM for i in range(len(ins))],
+        in_specs=[HBM if i in in_hbm else VMEM for i in range(len(ins))],
         out_specs=tuple(HBM if i in out_hbm else VMEM for i in range(len(outs))),
         scratch_shapes=list(scratch),
         input_output_aliases=alias or {},
@@ -397,8 +405,6 @@
     half, quarter = extent // 2, extent // 4
     rows, cols = lax.axis_size("row"), lax.axis_size("col")
     sides = 1 if rows == 2 else 2
-    row, col = lax.axis_index("row"), lax.axis_index("col")
-    par = jnp.stack([row & 1, col & 1, (col >> 1) & 1, (col >> 2) & 1]).astype(jnp.int32)
     offsets = positions.reshape(-1, 2)
     count = offsets.shape[0]
     measured_in = intensity.reshape(-1, extent, extent)
@@ -411,47 +417,49 @@
     obj, *sent = call(
         pack_kernel,
         [obj_in.shape] + [(extent, LANES)] * 2 + [(PLANES * RIM, extent)] * sides,
-        (par, obj_in),
+        (obj_in,),
         scratch=[pltpu.SemaphoreType.DMA((PLANES,))],
-        in_hbm=(1,),
+        in_hbm=(0,),
     )
     col2 = pairs(sent[1], "col", 1)
     col1 = pairs(sent[0], "col", 0)
     row_in = [pairs(sent[2 + n], "row", n) for n in range(sides)]
-    probe, measured, mats, window, mask2, mask4 = call(
+    probe, measured, mats, window, grad, mask2, mask4 = call(
         prep_kernel,
         [
             probe_in.shape,
             measured_in.shape,
             jax.ShapeDtypeStruct((4, 2, 2 * extent, 2 * extent), bf16),
             (PLANES, tiles + 2, span, LANES),
+            (PLANES, tiles + 2, span, LANES),
             (half, extent),
             (quarter, extent),
         ],
-        (par, obj, probe_in, measured_in, tabs),
+        (obj, probe_in, measured_in, tabs),
         scratch=[pltpu.VMEM(tabs.shape, bf16), pltpu.SemaphoreType.DMA((3,))],
-        in_hbm=(2, 3, 4),
+        in_hbm=(1, 2, 3),
         limit=16,
     )
-    corners = call(corner_kernel, [(2 * RIM, LANES)] * sides, (par, col1, col2))
+    corners = call(corner_kernel, [(2 * RIM, LANES)] * sides, (col1, col2))
     corner_in = [pairs(corners[n], "row", n) for n in range(sides)]
 
-    ins = (offsets, par, col1, col2, *row_in, *corner_in, probe, measured, mats, window)
+    ins = (offsets, col1, col2, *row_in, *corner_in, probe, measured, mats, window, grad)
     shapes = [(extent + rim_rows, extent)] + [(rim_rows, extent)] * (sides - 1)
-    shapes += [(extent, extent), (PLANES, extent, extent), (extent, LANES), (extent, LANES), window.shape]
+    shapes += [(extent, extent), (PLANES, extent, extent), (extent, LANES), (extent, LANES), window.shape, grad.shape]
     out = call(
         functools.partial(tile_kernel, sides),
         shapes,
         ins,
         scratch=[
-            pltpu.VMEM((PLANES, tiles + 2, span, LANES), f32),
             pltpu.VMEM((count, PLANES, extent, extent), f32),
             pltpu.VMEM((count, 2, extent, extent), f32),
             pltpu.VMEM((2, count * extent, 2 * extent), bf16),
             pltpu.VMEM((2, 2 * extent, count * extent), bf16),
+            pltpu.SMEM(offsets.shape, jnp.int32),
+            pltpu.SemaphoreType.DMA,
         ],
-        smem=2,
-        alias={len(ins) - 1: len(shapes) - 1},
+        in_hbm=(0,),
+        alias={len(ins) - 2: len(shapes) - 2, len(ins) - 1: len(shapes) - 1},
         limit=32,
     )
     row_back = [pairs(out[n], "row", n) for n in range(sides)]
@@ -459,18 +467,18 @@
     probe_msg, probe_keep, msg1, msg2 = call(
         functools.partial(cols_kernel, sides),
         [(half, extent)] * 4,
-        (par, keep, left, right, *row_back),
+        (keep, left, right, *row_back),
         scratch=[pltpu.VMEM((2, extent, LANES), f32)],
     )
     probe_got = swap(probe_msg, "col", 2)
     got2 = pairs(msg2, "col", 1)
     got1 = pairs(msg1, "col", 0)
-    keep3, send3 = call(split_kernel, [(quarter, extent)] * 2, (par, probe_keep, probe_got))
+    keep3, send3 = call(split_kernel, [(quarter, extent)] * 2, (probe_keep, probe_got))
     got3 = swap(send3, "col", 4)
     state, descent = call(
         functools.partial(gather_kernel, sides),
         [(quarter + 8, extent), (PLANES, extent, extent)],
-        (par, inner, keep3, got3, got1, got2, *row_back),
+        (inner, keep3, got3, got1, got2, *row_back),
     )
     is_sum = lax.broadcasted_iota(jnp.int32, state.shape, 0) < quarter
     steps = [("col", 1 << b) for b in range(3, cols.bit_length() - 1)] + [("col", 1)]
@@ -492,7 +500,7 @@
     object_out, probe_out = call(
         functools.partial(final_kernel, 2.0 / (rows * cols)),
         [obj.shape, probe_in.shape],
-        (par, obj, descent, probe, state, other),
+        (obj, descent, probe, state, other),
         scratch=[pltpu.VMEM((PLANES + 2, extent, extent), f32), pltpu.SemaphoreType.DMA((PLANES + 2,))],
         out_hbm=(0, 1),
     )

time: 64.8 us -> 61.2 us (0.944)
  Pallas kernels: 18.1 us -> 14.1 us
  waiting for transfers between devices: 23.8 us -> 24.7 us
    pallas_call x8, Pallas kernels: 18.1 us -> 14.1 us  [call(): pl.pallas_call(kernel, out_shape=tuple(shapes), in_specs=[HBM if i in in_...]
    ppermute x7, waiting for transfers between devices: 19.7 us -> 20.6 us  [swap(): return lax.ppermute(value, axis, [(i, i ^ bit) for i in range(count)])]
  transfers between devices with their start and end apart: 14 -> 14, of which waited for: 9 -> 9; matrix products, arithmetic and copies ran while one was open for 0% -> 0% of each run, Pallas kernels for 5% -> 3%
where the time goes in v3:
time: 61.2 us; the launch traced here: 61 us
  waiting for transfers between devices  24.7 us (40%)
  starting transfers between devices  21.1 us (34%)
  Pallas kernels  14.1 us (23%)
  between operations  0.78 us (1%)
    ppermute x7, waiting for transfers between devices, swap(): return lax.ppermute(value, axis, [(i, i ^ bit) for i in range(count)])  20.6 us
    ppermute x7, starting transfers between devices, swap(): return lax.ppermute(value, axis, [(i, i ^ bit) for i in range(count)])  14.7 us
    pallas_call x8, Pallas kernels, call(): pl.pallas_call(kernel, out_shape=tuple(shapes), in_specs=[HBM if i in in_...  14.1 us
    ppermute x7, starting transfers between devices, pairs(): return lax.ppermute(value, axis, links)  6.39 us
    ppermute x7, waiting for transfers between devices, pairs(): return lax.ppermute(value, axis, links)  4.16 us
  transfers between devices with their start and end apart: 14, of which 9 were waited for; matrix products, arithmetic and copies ran while one was open for 0% of the time, Pallas kernels for 3%

profile of v3, /device:TPU:0, one launch (start us, length us, event | category | flops | bytes accessed | tf_op | source)
XLA Modules:
  0.0 61.0 jit_solution(9270839660665128569)
XLA Ops:
  0.6 1.5 %shard_map.68 = (f32[4,256,256]{2,1,0:T(8,128)S(1)}, f32[256,128]{1,0:T(8,128)S(1)}, f32[256,128]{1,0:T(8,128)S(1)}, f32[128,256]{1,0:T(8,128)S(1)}) custom-call(f32[4,256,256]{2,1,0:T(8,128)} %bitcast.4), custom_call_target="tpu_custom_call" | custom-call | tf_op jit(solution)/shard_map/pallas_call | solution.py:379
  2.1 3.0 %collective-permute-start = (f32[256,128]{1,0:T(8,128)S(1)}, f32[256,128]{1,0:T(8,128)S(1)}, u32[]{:S(2)}, u32[]{:S(2)}) collective-permute-start(f32[256,128]{1,0:T(8,128)S(1)} %get-tuple-element.29), channel_id=1, source_target_pairs={{0,1},{1,0},{2,3},{3,2},{4,5},{5,4},{6,7},{7,6},{8,9},{9,8},{10,11... | collective-permute-start | bytes 393224 | tf_op jit(solution)/shard_map/ppermute | solution.py:400
  5.1 0.7 %collective-permute-start.1 = (f32[256,128]{1,0:T(8,128)S(1)}, f32[256,128]{1,0:T(8,128)S(1)}, u32[]{:S(2)}, u32[]{:S(2)}) collective-permute-start(f32[256,128]{1,0:T(8,128)S(1)} %get-tuple-element.30), channel_id=1, source_target_pairs={{1,2},{2,1},{3,4},{4,3},{5,6},{6,5},{7,8},{8,7},{9,10},{10,9},{11,... | collective-permute-start | bytes 393224 | tf_op jit(solution)/shard_map/ppermute | solution.py:400
  5.8 0.1 collective-permute-start.2
  5.9 2.8 %collective-permute-done.col1 = f32[256,128]{1,0:T(8,128)S(1)} collective-permute-done((f32[256,128]{1,0:T(8,128)S(1)}, f32[256,128]{1,0:T(8,128)S(1)}, u32[]{:S(2)}, u32[]{:S(2)}) %collective-permute-start) | collective-permute-done | bytes 131104 | tf_op jit(solution)/shard_map/ppermute | solution.py:400
  8.6 0.0 collective-permute-done.1.col2
  8.6 0.0 collective-permute-start.3
  8.7 1.5 %shard_map.70 = (f32[2,256,256]{2,1,0:T(8,128)S(1)}, f32[2,256,256]{2,1,0:T(8,128)S(1)}, bf16[4,2,512,512]{3,2,1,0:T(8,128)(2,1)S(1)}, f32[4,4,320,128]{3,2,1,0:...) custom-call(f32[4,256,256]{2,1,0:T(8,128)S(1)} %get-tuple-element.28.obj, ...), custom_call_target="tpu_custom_call" | custom-call | tf_op jit(solution)/shard_map/pallas_call | solution.py:379
  10.2 0.0 collective-permute-done.2.rest_0_
  10.2 0.0 collective-permute-done.3.rest_1_
  10.2 9.4 %shard_map.71 = (f32[416,256]{1,0:T(8,128)S(1)}, f32[256,256]{1,0:T(8,128)S(1)}, f32[4,256,256]{2,1,0:T(8,128)S(1)}, f32[256,128]{1,0:T(8,128)S(1)}, f32[256,128...) custom-call(s32[2,2]{1,0:T(2,128)} %bitcast.6, ...), custom_call_target="tpu_custom_call", output_to_operand_aliasing={{5}: (8, {}), {6}: (9, {})} | custom-call | tf_op jit(solution)/shard_map/pallas_call | solution.py:379
  19.6 0.6 collective-permute-start.4
  20.2 1.4 %collective-permute-done.4.rest_0_ = f32[416,256]{1,0:T(8,128)S(1)} collective-permute-done((f32[416,256]{1,0:T(8,128)S(1)}, f32[416,256]{1,0:T(8,128)S(1)}, u32[]{:S(2)}, u32[]{:S(2)}) %collective-permute-start.4) | collective-permute-done | bytes 426016 | tf_op jit(solution)/shard_map/ppermute | solution.py:400
  21.6 0.1 shard_map.72
  21.7 5.9 %collective-permute-start.5 = (f32[128,256]{1,0:T(8,128)S(1)}, f32[128,256]{1,0:T(8,128)S(1)}, u32[]{:S(2)}, u32[]{:S(2)}) collective-permute-start(f32[128,256]{1,0:T(8,128)S(1)} %get-tuple-element.43), channel_id=1, source_target_pairs={{0,2},{1,3},{2,0},{3,1},{4,6},{5,7},{6,4},{7,5},{8,10},{9,11},{10,... | collective-permute-start | bytes 393224 | tf_op jit(solution)/shard_map/ppermute | solution.py:392
  27.6 1.4 %collective-permute-start.7 = (f32[128,256]{1,0:T(8,128)S(1)}, f32[128,256]{1,0:T(8,128)S(1)}, u32[]{:S(2)}, u32[]{:S(2)}) collective-permute-start(f32[128,256]{1,0:T(8,128)S(1)} %get-tuple-element.46), channel_id=1, source_target_pairs={{0,1},{1,0},{2,3},{3,2},{4,5},{5,4},{6,7},{7,6},{8,9},{9,8},{10,11... | collective-permute-start | bytes 393224 | tf_op jit(solution)/shard_map/ppermute | solution.py:400
  29.0 0.7 %collective-permute-start.8 = (f32[128,256]{1,0:T(8,128)S(1)}, f32[128,256]{1,0:T(8,128)S(1)}, u32[]{:S(2)}, u32[]{:S(2)}) collective-permute-start(f32[128,256]{1,0:T(8,128)S(1)} %get-tuple-element.47), channel_id=1, source_target_pairs={{1,2},{2,1},{3,4},{4,3},{5,6},{6,5},{7,8},{8,7},{9,10},{10,9},{11,... | collective-permute-start | bytes 393224 | tf_op jit(solution)/shard_map/ppermute | solution.py:400
  29.7 2.0 %collective-permute-done.5.other = f32[128,256]{1,0:T(8,128)S(1)} collective-permute-done((f32[128,256]{1,0:T(8,128)S(1)}, f32[128,256]{1,0:T(8,128)S(1)}, u32[]{:S(2)}, u32[]{:S(2)}) %collective-permute-start.5) | collective-permute-done | bytes 131104 | tf_op jit(solution)/shard_map/ppermute | solution.py:392
  31.6 2.7 %collective-permute-start.6 = (f32[64,256]{1,0:T(8,128)S(1)}, f32[64,256]{1,0:T(8,128)S(1)}, u32[]{:S(2)}, u32[]{:S(2)}) collective-permute-start(f32[64,256]{1,0:T(8,128)S(1)} %get-tuple-element.45), channel_id=1, source_target_pairs={{0,4},{1,5},{2,6},{3,7},{4,0},{5,1},{6,2},{7,3},{8,12},{9,13},{10,... | collective-permute-start | bytes 196616 | tf_op jit(solution)/shard_map/ppermute | solution.py:392
  34.3 0.0 collective-permute-done.7.col1
  34.3 0.0 collective-permute-done.8.col2
  34.3 3.0 %collective-permute-done.6.got3 = f32[64,256]{1,0:T(8,128)S(1)} collective-permute-done((f32[64,256]{1,0:T(8,128)S(1)}, f32[64,256]{1,0:T(8,128)S(1)}, u32[]{:S(2)}, u32[]{:S(2)}) %collective-permute-start.6) | collective-permute-done | bytes 65568 | tf_op jit(solution)/shard_map/ppermute | solution.py:392
  37.4 0.3 shard_map.74
  37.7 3.6 %collective-permute-start.9 = (f32[72,256]{1,0:T(8,128)S(1)}, f32[72,256]{1,0:T(8,128)S(1)}, u32[]{:S(2)}, u32[]{:S(2)}) collective-permute-start(f32[72,256]{1,0:T(8,128)S(1)} %get-tuple-element.51), channel_id=1, source_target_pairs={{0,8},{1,9},{2,10},{3,11},{4,12},{5,13},{6,14},{7,15},{8,0},{9,1},... | collective-permute-start | bytes 221192 | tf_op jit(solution)/shard_map/ppermute | solution.py:392
  41.4 2.3 %collective-permute-done.9 = f32[72,256]{1,0:T(8,128)S(1)} collective-permute-done((f32[72,256]{1,0:T(8,128)S(1)}, f32[72,256]{1,0:T(8,128)S(1)}, u32[]{:S(2)}, u32[]{:S(2)}) %collective-permute-start.9) | collective-permute-done | bytes 73760 | tf_op jit(solution)/shard_map/ppermute | solution.py:392
  43.7 0.1 maximum_select_fusion.1
  43.8 0.1 collective-permute-start.10
  43.8 4.3 %collective-permute-done.10 = f32[72,256]{1,0:T(8,128)S(1)} collective-permute-done((f32[72,256]{1,0:T(8,128)S(1)}, f32[72,256]{1,0:T(8,128)S(1)}, u32[]{:S(2)}, u32[]{:S(2)}) %collective-permute-start.10) | collective-permute-done | bytes 73760 | tf_op jit(solution)/shard_map/ppermute | solution.py:392
  48.2 0.1 maximum_select_fusion
  48.3 2.2 %collective-permute-start.11 = (f32[72,256]{1,0:T(8,128)S(1)}, f32[72,256]{1,0:T(8,128)S(1)}, u32[]{:S(2)}, u32[]{:S(2)}) collective-permute-start(f32[72,256]{1,0:T(8,128)S(1)} %maximum_select_fusion), channel_id=1, source_target_pairs={{0,4},{1,5},{2,6},{3,7},{4,0},{5,1},{6,2},{7,3},{8,12},{9,13},{10,... | collective-permute-start | bytes 221192 | tf_op jit(solution)/shard_map/ppermute | solution.py:392
  50.5 2.3 %collective-permute-done.11 = f32[72,256]{1,0:T(8,128)S(1)} collective-permute-done((f32[72,256]{1,0:T(8,128)S(1)}, f32[72,256]{1,0:T(8,128)S(1)}, u32[]{:S(2)}, u32[]{:S(2)}) %collective-permute-start.11) | collective-permute-done | bytes 73760 | tf_op jit(solution)/shard_map/ppermute | solution.py:392
  52.9 0.1 collective-permute-start.12
  53.0 5.0 %collective-permute-done.12 = f32[136,256]{1,0:T(8,128)S(1)} collective-permute-done((f32[136,256]{1,0:T(8,128)S(1)}, f32[136,256]{1,0:T(8,128)S(1)}, u32[]{:S(2)}, u32[]{:S(2)}) %collective-permute-start.12) | collective-permute-done | bytes 139296 | tf_op jit(solution)/shard_map/ppermute | solution.py:392
  58.1 0.1 collective-permute-start.13
  58.2 1.5 %collective-permute-done.13.other = f32[264,256]{1,0:T(8,128)S(1)} collective-permute-done((f32[264,256]{1,0:T(8,128)S(1)}, f32[264,256]{1,0:T(8,128)S(1)}, u32[]{:S(2)}, u32[]{:S(2)}) %collective-permute-start.13) | collective-permute-done | bytes 270368 | tf_op jit(solution)/shard_map/ppermute | solution.py:392
  59.7 1.3 %shard_map.75 = (f32[4,256,256]{2,1,0:T(8,128)}, f32[2,256,256]{2,1,0:T(8,128)}) custom-call(f32[4,256,256]{2,1,0:T(8,128)S(1)} %get-tuple-element.28.obj, f32[4,256,256]{2,1,0:T(8,128)S(1)} %get-tuple-element.48.descent, f32[2,256,256]{2,1,0:T(8,128)S(1)} %get-tuple-element.32.rest_2_.probe, f32[264,256]{1,0:T(8,128)S(1)} %pad_maximum_fusion.mine, ...), custom_call_target="tpu_custom_call" | custom-call | tf_op jit(solution)/shard_map/pallas_call | solution.py:379
  (11 shorter events, 0.1 us)
Async XLA Ops:
  2.1 6.5 %collective-permute-start = (f32[256,128]{1,0:T(8,128)S(1)}, f32[256,128]{1,0:T(8,128)S(1)}, u32[]{:S(2)}, u32[]{:S(2)}) collective-permute-start(f32[256,128]{1,0:T(8,128)S(1)} %get-tuple-element.29), channel_id=1, source_target_pairs={{0,1},{1,0},{2,3},{3,2},{4,5},{5,4},{6,7},{7,6},{8,9},{9,8},{10,11... | collective-permute-start | bytes 393224 | tf_op jit(solution)/shard_map/ppermute | solution.py:400
  5.1 3.5 %collective-permute-start.1 = (f32[256,128]{1,0:T(8,128)S(1)}, f32[256,128]{1,0:T(8,128)S(1)}, u32[]{:S(2)}, u32[]{:S(2)}) collective-permute-start(f32[256,128]{1,0:T(8,128)S(1)} %get-tuple-element.30), channel_id=1, source_target_pairs={{1,2},{2,1},{3,4},{4,3},{5,6},{6,5},{7,8},{8,7},{9,10},{10,9},{11,... | collective-permute-start | bytes 393224 | tf_op jit(solution)/shard_map/ppermute | solution.py:400
  5.8 4.4 %collective-permute-start.2 = (f32[128,256]{1,0:T(8,128)S(1)}, f32[128,256]{1,0:T(8,128)S(1)}, u32[]{:S(2)}, u32[]{:S(2)}) collective-permute-start(f32[128,256]{1,0:T(8,128)S(1)} %get-tuple-element.31), channel_id=1, source_target_pairs={{0,16},{16,0},{1,17},{17,1},{2,18},{18,2},{3,19},{19,3},{4,20},{20... | collective-permute-start | bytes 393224 | tf_op jit(solution)/shard_map/ppermute | solution.py:400
  8.6 1.6 %collective-permute-start.3 = (f32[64,128]{1,0:T(8,128)S(1)}, f32[64,128]{1,0:T(8,128)S(1)}, u32[]{:S(2)}, u32[]{:S(2)}) collective-permute-start(f32[64,128]{1,0:T(8,128)S(1)} %shard_map.69), channel_id=1, source_target_pairs={{0,16},{16,0},{1,17},{17,1},{2,18},{18,2},{3,19},{19,3},{4,20},{20... | collective-permute-start | bytes 98312 | tf_op jit(solution)/shard_map/ppermute | solution.py:400
  19.6 2.0 %collective-permute-start.4 = (f32[416,256]{1,0:T(8,128)S(1)}, f32[416,256]{1,0:T(8,128)S(1)}, u32[]{:S(2)}, u32[]{:S(2)}) collective-permute-start(f32[416,256]{1,0:T(8,128)S(1)} %get-tuple-element.41), channel_id=1, source_target_pairs={{0,16},{16,0},{1,17},{17,1},{2,18},{18,2},{3,19},{19,3},{4,20},{20... | collective-permute-start | bytes 1277960 | tf_op jit(solution)/shard_map/ppermute | solution.py:400
  21.7 10.0 %collective-permute-start.5 = (f32[128,256]{1,0:T(8,128)S(1)}, f32[128,256]{1,0:T(8,128)S(1)}, u32[]{:S(2)}, u32[]{:S(2)}) collective-permute-start(f32[128,256]{1,0:T(8,128)S(1)} %get-tuple-element.43), channel_id=1, source_target_pairs={{0,2},{1,3},{2,0},{3,1},{4,6},{5,7},{6,4},{7,5},{8,10},{9,11},{10,... | collective-permute-start | bytes 393224 | tf_op jit(solution)/shard_map/ppermute | solution.py:392
  27.6 6.7 %collective-permute-start.7 = (f32[128,256]{1,0:T(8,128)S(1)}, f32[128,256]{1,0:T(8,128)S(1)}, u32[]{:S(2)}, u32[]{:S(2)}) collective-permute-start(f32[128,256]{1,0:T(8,128)S(1)} %get-tuple-element.46), channel_id=1, source_target_pairs={{0,1},{1,0},{2,3},{3,2},{4,5},{5,4},{6,7},{7,6},{8,9},{9,8},{10,11... | collective-permute-start | bytes 393224 | tf_op jit(solution)/shard_map/ppermute | solution.py:400
  29.0 5.3 %collective-permute-start.8 = (f32[128,256]{1,0:T(8,128)S(1)}, f32[128,256]{1,0:T(8,128)S(1)}, u32[]{:S(2)}, u32[]{:S(2)}) collective-permute-start(f32[128,256]{1,0:T(8,128)S(1)} %get-tuple-element.47), channel_id=1, source_target_pairs={{1,2},{2,1},{3,4},{4,3},{5,6},{6,5},{7,8},{8,7},{9,10},{10,9},{11,... | collective-permute-start | bytes 393224 | tf_op jit(solution)/shard_map/ppermute | solution.py:400
  31.6 5.7 %collective-permute-start.6 = (f32[64,256]{1,0:T(8,128)S(1)}, f32[64,256]{1,0:T(8,128)S(1)}, u32[]{:S(2)}, u32[]{:S(2)}) collective-permute-start(f32[64,256]{1,0:T(8,128)S(1)} %get-tuple-element.45), channel_id=1, source_target_pairs={{0,4},{1,5},{2,6},{3,7},{4,0},{5,1},{6,2},{7,3},{8,12},{9,13},{10,... | collective-permute-start | bytes 196616 | tf_op jit(solution)/shard_map/ppermute | solution.py:392
  37.7 6.0 %collective-permute-start.9 = (f32[72,256]{1,0:T(8,128)S(1)}, f32[72,256]{1,0:T(8,128)S(1)}, u32[]{:S(2)}, u32[]{:S(2)}) collective-permute-start(f32[72,256]{1,0:T(8,128)S(1)} %get-tuple-element.51), channel_id=1, source_target_pairs={{0,8},{1,9},{2,10},{3,11},{4,12},{5,13},{6,14},{7,15},{8,0},{9,1},... | collective-permute-start | bytes 221192 | tf_op jit(solution)/shard_map/ppermute | solution.py:392
  43.8 4.4 %collective-permute-start.10 = (f32[72,256]{1,0:T(8,128)S(1)}, f32[72,256]{1,0:T(8,128)S(1)}, u32[]{:S(2)}, u32[]{:S(2)}) collective-permute-start(f32[72,256]{1,0:T(8,128)S(1)} %maximum_select_fusion.1), channel_id=1, source_target_pairs={{0,1},{1,0},{2,3},{3,2},{4,5},{5,4},{6,7},{7,6},{8,9},{9,8},{10,11... | collective-permute-start | bytes 221192 | tf_op jit(solution)/shard_map/ppermute | solution.py:392
  48.3 4.6 %collective-permute-start.11 = (f32[72,256]{1,0:T(8,128)S(1)}, f32[72,256]{1,0:T(8,128)S(1)}, u32[]{:S(2)}, u32[]{:S(2)}) collective-permute-start(f32[72,256]{1,0:T(8,128)S(1)} %maximum_select_fusion), channel_id=1, source_target_pairs={{0,4},{1,5},{2,6},{3,7},{4,0},{5,1},{6,2},{7,3},{8,12},{9,13},{10,... | collective-permute-start | bytes 221192 | tf_op jit(solution)/shard_map/ppermute | solution.py:392
  52.9 5.1 %collective-permute-start.12 = (f32[136,256]{1,0:T(8,128)S(1)}, f32[136,256]{1,0:T(8,128)S(1)}, u32[]{:S(2)}, u32[]{:S(2)}) collective-permute-start(f32[136,256]{1,0:T(8,128)S(1)} %pad_maximum_fusion.1), channel_id=1, source_target_pairs={{0,2},{1,3},{2,0},{3,1},{4,6},{5,7},{6,4},{7,5},{8,10},{9,11},{10,... | collective-permute-start | bytes 417800 | tf_op jit(solution)/shard_map/ppermute | solution.py:392
  58.1 1.6 %collective-permute-start.13 = (f32[264,256]{1,0:T(8,128)S(1)}, f32[264,256]{1,0:T(8,128)S(1)}, u32[]{:S(2)}, u32[]{:S(2)}) collective-permute-start(f32[264,256]{1,0:T(8,128)S(1)} %pad_maximum_fusion.mine), channel_id=1, source_target_pairs={{0,16},{16,0},{1,17},{17,1},{2,18},{18,2},{3,19},{19,3},{4,20},{20... | collective-permute-start | bytes 811016 | tf_op jit(solution)/shard_map/ppermute | solution.py:392

commit v4 on v3

--- a/solution.py
+++ b/solution.py
@@ -84,7 +84,7 @@
             msg[RIM * q : RIM * (q + 1), :] = obj[q, pl.ds(start, RIM), :]
 
 
-def prep_kernel(obj, probe_hbm, measured_hbm, tabs_hbm, probe, measured, mats, window, grad, mask2, mask4, tabs, sem):
+def prep_kernel(obj, probe_hbm, measured_hbm, tabs_hbm, pos_hbm, probe, measured, mats, window, grad, mask2, mask4, pos, tabs, sem):
     extent = obj.shape[-1]
     tiles = extent // LANES
     par = parities()
@@ -92,6 +92,7 @@
         pltpu.make_async_copy(tabs_hbm, tabs, sem.at[0]),
         pltpu.make_async_copy(probe_hbm, probe, sem.at[1]),
         pltpu.make_async_copy(measured_hbm, measured, sem.at[2]),
+        pltpu.make_async_copy(pos_hbm, pos, sem.at[3]),
     ]
     for copy in copies:
         copy.start()
@@ -117,11 +118,11 @@
             mats[index, part, extent:, extent:] = diag
             mats[index, part, :extent, extent:] = upper
             mats[index, part, extent:, :extent] = lower
-    copies[1].wait()
-    copies[2].wait()
-
-
-def tile_kernel(sides, pos_hbm, col1, col2, *rest):
+    for copy in copies[1:]:
+        copy.wait()
+
+
+def tile_kernel(sides, pos_in, col1, col2, *rest):
     row_in = rest[:sides]
     corner_in = rest[sides : 2 * sides]
     probe, measured, mats = rest[2 * sides : 2 * sides + 3]
@@ -129,7 +130,7 @@
     row_out = outs[:sides]
     keep_out, inner_out, left_out, right_out, window, grad = outs[sides : sides + 6]
     patch, wave, right_in, left_in, pos, sem = outs[sides + 6 :]
-    fetch = pltpu.make_async_copy(pos_hbm, pos, sem)
+    fetch = pltpu.make_async_copy(pos_in, pos, sem)
     fetch.start()
     par = parities()
     extent = probe.shape[-1]
@@ -173,21 +174,23 @@
             right_in[0, cols(p), cols(c)] = high
             right_in[1, cols(p), cols(c)] = low
 
-    def right_stage(index):
+    def right_stage(index, p):
         for c in range(2):
-            both = jnp.dot(right_in[0], mats[index, 0, :, cols(c)], preferred_element_type=f32)
-            both += jnp.dot(right_in[0], mats[index, 1, :, cols(c)], preferred_element_type=f32)
-            both += jnp.dot(right_in[1], mats[index, 0, :, cols(c)], preferred_element_type=f32)
-            for p in range(count):
-                high, low = split(both[cols(p)])
-                left_in[0, cols(c), cols(p)] = high
-                left_in[1, cols(c), cols(p)] = low
+            part = jnp.dot(right_in[0, cols(p), :], mats[index, 0, :, cols(c)], preferred_element_type=f32)
+            part += jnp.dot(right_in[0, cols(p), :], mats[index, 1, :, cols(c)], preferred_element_type=f32)
+            part += jnp.dot(right_in[1, cols(p), :], mats[index, 0, :, cols(c)], preferred_element_type=f32)
+            high, low = split(part)
+            left_in[0, cols(c), cols(p)] = high
+            left_in[1, cols(c), cols(p)] = low
 
     def left_stage(index, p):
-        both = jnp.dot(mats[index, 0], left_in[0, :, cols(p)], preferred_element_type=f32)
-        both += jnp.dot(mats[index, 1], left_in[0, :, cols(p)], preferred_element_type=f32)
-        both += jnp.dot(mats[index, 0], left_in[1, :, cols(p)], preferred_element_type=f32)
-        return both[:extent], both[extent:]
+        out = []
+        for c in range(2):
+            part = jnp.dot(mats[index, 0, cols(c), :], left_in[0, :, cols(p)], preferred_element_type=f32)
+            part += jnp.dot(mats[index, 1, cols(c), :], left_in[0, :, cols(p)], preferred_element_type=f32)
+            part += jnp.dot(mats[index, 0, cols(c), :], left_in[1, :, cols(p)], preferred_element_type=f32)
+            out.append(part)
+        return out
 
     def add_piece(p, q, value):
         down, first, turn = place(p)
@@ -201,37 +204,70 @@
                 piece = jnp.where(lane >= turn, moved[t], moved[t - 1])
             grad[q, first + t, pl.ds(down, extent), :] += piece
 
-    for p in range(count):
+    def cut(p, planes):
         down, first, turn = place(p)
         back = (LANES - turn) % LANES
-        for q in range(PLANES):
+        for q in planes:
             got = [pltpu.roll(window[q, first + t, pl.ds(down, extent), :], back, 1) for t in range(tiles + 1)]
             for t in range(tiles):
                 patch[p, q, :, LANES * t : LANES * (t + 1)] = jnp.where(lane < LANES - turn, got[t], got[t + 1])
+
+    for p in range(count):
+        cut(p, (0, 1))
         pr, pi = probe[0], probe[1]
         ar, ai = patch[p, 0], patch[p, 1]
         to_right(p, pr * ar - pi * ai, pr * ai + pi * ar)
-    right_stage(0)
+        right_stage(0, p)
+    for p in range(count):
+        cut(p, (2, 3))
     for p in range(count):
         qr, qi = left_stage(1, p)
         wave[p, 0] = qr
         wave[p, 1] = qi
         br, bi = patch[p, 2], patch[p, 3]
         to_right(p, qr * br - qi * bi, qr * bi + qi * br)
-    right_stage(2)
+        right_stage(2, p)
     for p in range(count):
         fr, fi = left_stage(3, p)
         excess = 2.0 * (fr * fr + fi * fi - measured[p])
         to_right(p, excess * fr, excess * fi)
-    right_stage(3)
+        right_stage(3, p)
     for p in range(count):
         hr, hi = left_stage(2, p)
+        br, bi = patch[p, 2], patch[p, 3]
+        to_right(p, br * hr + bi * hi, br * hi - bi * hr)
+        right_stage(1, p)
         qr, qi = wave[p, 0], wave[p, 1]
         add_piece(p, 2, qr * hr + qi * hi)
         add_piece(p, 3, qr * hi - qi * hr)
-        br, bi = patch[p, 2], patch[p, 3]
-        to_right(p, br * hr + bi * hi, br * hi - bi * hr)
-    right_stage(1)
+
+    def packed(planes, old, tile, left, start, rows):
+        narrow = lanes_of(rows)
+        for q in planes:
+            value = grad[q, tile, pl.ds(start, rows), :]
+            turn = (RIM * q + (RIM if left else 0)) % LANES
+            value = pltpu.roll(value, turn, 1) if turn else value
+            old = value if old is None else jnp.where((narrow >= RIM * q) & (narrow < RIM * (q + 1)), value, old)
+        return old
+
+    def emit(planes, begin):
+        for ref, tile, left in ((left_out, 0, True), (right_out, tiles + 1, False)):
+            ref[...] = packed(planes, None if begin else ref[...], tile, left, RIM, extent)
+        for q in planes:
+            for t in range(tiles):
+                inner_out[q, :, LANES * t : LANES * (t + 1)] = grad[q, t + 1, RIM : RIM + extent, :]
+        for n in range(sides):
+            base = extent if n == 0 else 0
+            for q in planes:
+                for t in range(tiles):
+                    row_out[n][base + RIM * q : base + RIM * (q + 1), LANES * t : LANES * (t + 1)] = grad[q, t + 1, pl.ds(starts[n], RIM), :]
+            at = base + RIM * PLANES
+            for tile, left in ((0, True), (tiles + 1, False)):
+                where = slice(0, LANES) if left else slice(LANES, 2 * LANES)
+                old = None if begin else row_out[n][at : at + RIM, where]
+                row_out[n][at : at + RIM, where] = packed(planes, old, tile, left, starts[n], RIM)
+
+    emit((2, 3), True)
     for p in range(count):
         er, ei = left_stage(0, p)
         pr, pi = probe[0], probe[1]
@@ -248,30 +284,7 @@
     is_odd = odd_row == 1
     keep_out[...] = jnp.where(is_odd, wave[0, 1], wave[0, 0])
     row_out[0][:extent, :] = jnp.where(is_odd, wave[0, 0], wave[0, 1])
-
-    def packed(tile, left, start, rows):
-        out = jnp.zeros((rows, LANES), f32)
-        narrow = lanes_of(rows)
-        for q in range(PLANES):
-            value = grad[q, tile, pl.ds(start, rows), :]
-            turn = (RIM * q + (RIM if left else 0)) % LANES
-            value = pltpu.roll(value, turn, 1) if turn else value
-            out = jnp.where((narrow >= RIM * q) & (narrow < RIM * (q + 1)), value, out)
-        return out
-
-    left_out[...] = packed(0, True, RIM, extent)
-    right_out[...] = packed(tiles + 1, False, RIM, extent)
-    for q in range(PLANES):
-        for t in range(tiles):
-            inner_out[q, :, LANES * t : LANES * (t + 1)] = grad[q, t + 1, RIM : RIM + extent, :]
-    for n in range(sides):
-        base = extent if n == 0 else 0
-        for q in range(PLANES):
-            for t in range(tiles):
-                row_out[n][base + RIM * q : base + RIM * (q + 1), LANES * t : LANES * (t + 1)] = grad[q, t + 1, pl.ds(starts[n], RIM), :]
-        at = base + RIM * PLANES
-        row_out[n][at : at + RIM, :LANES] = packed(0, True, starts[n], RIM)
-        row_out[n][at : at + RIM, LANES : 2 * LANES] = packed(tiles + 1, False, starts[n], RIM)
+    emit((0, 1), False)
 
 
 def corner_kernel(col1, col2, *msgs):
@@ -405,8 +418,7 @@
     half, quarter = extent // 2, extent // 4
     rows, cols = lax.axis_size("row"), lax.axis_size("col")
     sides = 1 if rows == 2 else 2
-    offsets = positions.reshape(-1, 2)
-    count = offsets.shape[0]
+    count = positions.size // 2
     measured_in = intensity.reshape(-1, extent, extent)
     obj_in = object_in.reshape(PLANES, extent, extent)
     tabs = jnp.asarray(tables(extent))
@@ -424,7 +436,7 @@
     col2 = pairs(sent[1], "col", 1)
     col1 = pairs(sent[0], "col", 0)
     row_in = [pairs(sent[2 + n], "row", n) for n in range(sides)]
-    probe, measured, mats, window, grad, mask2, mask4 = call(
+    probe, measured, mats, window, grad, mask2, mask4, offsets = call(
         prep_kernel,
         [
             probe_in.shape,
@@ -434,10 +446,11 @@
             (PLANES, tiles + 2, span, LANES),
             (half, extent),
             (quarter, extent),
+            jax.ShapeDtypeStruct((count, 2), jnp.int32),
         ],
-        (obj, probe_in, measured_in, tabs),
-        scratch=[pltpu.VMEM(tabs.shape, bf16), pltpu.SemaphoreType.DMA((3,))],
-        in_hbm=(1, 2, 3),
+        (obj, probe_in, measured_in, tabs, positions.reshape(-1, 2)),
+        scratch=[pltpu.VMEM(tabs.shape, bf16), pltpu.SemaphoreType.DMA((4,))],
+        in_hbm=(1, 2, 3, 4),
         limit=16,
     )
     corners = call(corner_kernel, [(2 * RIM, LANES)] * sides, (col1, col2))
@@ -458,7 +471,6 @@
             pltpu.SMEM(offsets.shape, jnp.int32),
             pltpu.SemaphoreType.DMA,
         ],
-        in_hbm=(0,),
         alias={len(ins) - 2: len(shapes) - 2, len(ins) - 1: len(shapes) - 1},
         limit=32,
     )

time: 61.2 us -> 60.6 us (level)
  no operation moved by 1% of the time
where the time goes in v4:
time: 60.6 us; the launch traced here: 60.4 us
  waiting for transfers between devices  24.6 us (41%)
  starting transfers between devices  21.2 us (35%)
  Pallas kernels  13.6 us (22%)
  between operations  0.78 us (1%)
    ppermute x7, waiting for transfers between devices, swap(): return lax.ppermute(value, axis, [(i, i ^ bit) for i in range(count)])  20.4 us
    ppermute x7, starting transfers between devices, swap(): return lax.ppermute(value, axis, [(i, i ^ bit) for i in range(count)])  14.7 us
    pallas_call x8, Pallas kernels, call(): pl.pallas_call(kernel, out_shape=tuple(shapes), in_specs=[HBM if i in in_...  13.6 us
    ppermute x7, starting transfers between devices, pairs(): return lax.ppermute(value, axis, links)  6.45 us
    ppermute x7, waiting for transfers between devices, pairs(): return lax.ppermute(value, axis, links)  4.16 us
  transfers between devices with their start and end apart: 14, of which 9 were waited for; matrix products, arithmetic and copies ran while one was open for 0% of the time, Pallas kernels for 3%

profile of v4, /device:TPU:0, one launch (start us, length us, event | category | flops | bytes accessed | tf_op | source)
XLA Modules:
  0.0 60.4 jit_solution(17184030696060759555)
XLA Ops:
  0.6 1.5 %shard_map.68 = (f32[4,256,256]{2,1,0:T(8,128)S(1)}, f32[256,128]{1,0:T(8,128)S(1)}, f32[256,128]{1,0:T(8,128)S(1)}, f32[128,256]{1,0:T(8,128)S(1)}) custom-call(f32[4,256,256]{2,1,0:T(8,128)} %bitcast.4), custom_call_target="tpu_custom_call" | custom-call | tf_op jit(solution)/shard_map/pallas_call | solution.py:392
  2.1 3.0 %collective-permute-start = (f32[256,128]{1,0:T(8,128)S(1)}, f32[256,128]{1,0:T(8,128)S(1)}, u32[]{:S(2)}, u32[]{:S(2)}) collective-permute-start(f32[256,128]{1,0:T(8,128)S(1)} %get-tuple-element.31), channel_id=1, source_target_pairs={{0,1},{1,0},{2,3},{3,2},{4,5},{5,4},{6,7},{7,6},{8,9},{9,8},{10,11... | collective-permute-start | bytes 393224 | tf_op jit(solution)/shard_map/ppermute | solution.py:413
  5.1 0.7 %collective-permute-start.1 = (f32[256,128]{1,0:T(8,128)S(1)}, f32[256,128]{1,0:T(8,128)S(1)}, u32[]{:S(2)}, u32[]{:S(2)}) collective-permute-start(f32[256,128]{1,0:T(8,128)S(1)} %get-tuple-element.32), channel_id=1, source_target_pairs={{1,2},{2,1},{3,4},{4,3},{5,6},{6,5},{7,8},{8,7},{9,10},{10,9},{11,... | collective-permute-start | bytes 393224 | tf_op jit(solution)/shard_map/ppermute | solution.py:413
  5.8 0.1 collective-permute-start.2
  5.9 2.8 %collective-permute-done.col1 = f32[256,128]{1,0:T(8,128)S(1)} collective-permute-done((f32[256,128]{1,0:T(8,128)S(1)}, f32[256,128]{1,0:T(8,128)S(1)}, u32[]{:S(2)}, u32[]{:S(2)}) %collective-permute-start) | collective-permute-done | bytes 131104 | tf_op jit(solution)/shard_map/ppermute | solution.py:413
  8.6 0.0 collective-permute-done.1.col2
  8.6 0.0 collective-permute-start.3
  8.7 1.6 %shard_map.69 = (f32[2,256,256]{2,1,0:T(8,128)S(1)}, f32[2,256,256]{2,1,0:T(8,128)S(1)}, bf16[4,2,512,512]{3,2,1,0:T(8,128)(2,1)S(1)}, f32[4,4,320,128]{3,2,1,0:...) custom-call(f32[4,256,256]{2,1,0:T(8,128)S(1)} %get-tuple-element.29, ...), custom_call_target="tpu_custom_call" | custom-call | tf_op jit(solution)/shard_map/pallas_call | solution.py:392
  10.2 0.0 collective-permute-done.2.rest_0_
  10.2 0.0 collective-permute-done.3.rest_1_
  10.2 8.8 %shard_map.71 = (f32[416,256]{1,0:T(8,128)S(1)}, f32[256,256]{1,0:T(8,128)S(1)}, f32[4,256,256]{2,1,0:T(8,128)S(1)}, f32[256,128]{1,0:T(8,128)S(1)}, f32[256,128...) custom-call(s32[2,2]{1,0:T(2,128)S(1)} %get-tuple-element.30.pos_in,, ...), custom_call_target="tpu_custom_call", output_to_operand_aliasing={{5}: (8, {}), {6}: (9, {})} | custom-call | tf_op jit(solution)/shard_map/pallas_call | solution.py:392
  19.1 0.6 collective-permute-start.4
  19.7 1.4 %collective-permute-done.4.rest_0_ = f32[416,256]{1,0:T(8,128)S(1)} collective-permute-done((f32[416,256]{1,0:T(8,128)S(1)}, f32[416,256]{1,0:T(8,128)S(1)}, u32[]{:S(2)}, u32[]{:S(2)}) %collective-permute-start.4) | collective-permute-done | bytes 426016 | tf_op jit(solution)/shard_map/ppermute | solution.py:413
  21.1 0.1 shard_map.72
  21.1 5.9 %collective-permute-start.5 = (f32[128,256]{1,0:T(8,128)S(1)}, f32[128,256]{1,0:T(8,128)S(1)}, u32[]{:S(2)}, u32[]{:S(2)}) collective-permute-start(f32[128,256]{1,0:T(8,128)S(1)} %get-tuple-element.45), channel_id=1, source_target_pairs={{0,2},{1,3},{2,0},{3,1},{4,6},{5,7},{6,4},{7,5},{8,10},{9,11},{10,... | collective-permute-start | bytes 393224 | tf_op jit(solution)/shard_map/ppermute | solution.py:405
  27.0 1.5 %collective-permute-start.7 = (f32[128,256]{1,0:T(8,128)S(1)}, f32[128,256]{1,0:T(8,128)S(1)}, u32[]{:S(2)}, u32[]{:S(2)}) collective-permute-start(f32[128,256]{1,0:T(8,128)S(1)} %get-tuple-element.48), channel_id=1, source_target_pairs={{0,1},{1,0},{2,3},{3,2},{4,5},{5,4},{6,7},{7,6},{8,9},{9,8},{10,11... | collective-permute-start | bytes 393224 | tf_op jit(solution)/shard_map/ppermute | solution.py:413
  28.4 0.7 %collective-permute-start.8 = (f32[128,256]{1,0:T(8,128)S(1)}, f32[128,256]{1,0:T(8,128)S(1)}, u32[]{:S(2)}, u32[]{:S(2)}) collective-permute-start(f32[128,256]{1,0:T(8,128)S(1)} %get-tuple-element.49), channel_id=1, source_target_pairs={{1,2},{2,1},{3,4},{4,3},{5,6},{6,5},{7,8},{8,7},{9,10},{10,9},{11,... | collective-permute-start | bytes 393224 | tf_op jit(solution)/shard_map/ppermute | solution.py:413
  29.1 1.9 %collective-permute-done.5.other = f32[128,256]{1,0:T(8,128)S(1)} collective-permute-done((f32[128,256]{1,0:T(8,128)S(1)}, f32[128,256]{1,0:T(8,128)S(1)}, u32[]{:S(2)}, u32[]{:S(2)}) %collective-permute-start.5) | collective-permute-done | bytes 131104 | tf_op jit(solution)/shard_map/ppermute | solution.py:405
  31.1 2.7 %collective-permute-start.6 = (f32[64,256]{1,0:T(8,128)S(1)}, f32[64,256]{1,0:T(8,128)S(1)}, u32[]{:S(2)}, u32[]{:S(2)}) collective-permute-start(f32[64,256]{1,0:T(8,128)S(1)} %get-tuple-element.47), channel_id=1, source_target_pairs={{0,4},{1,5},{2,6},{3,7},{4,0},{5,1},{6,2},{7,3},{8,12},{9,13},{10,... | collective-permute-start | bytes 196616 | tf_op jit(solution)/shard_map/ppermute | solution.py:405
  33.8 0.0 collective-permute-done.7.col1
  33.8 0.0 collective-permute-done.8.col2
  33.8 3.0 %collective-permute-done.6.got3 = f32[64,256]{1,0:T(8,128)S(1)} collective-permute-done((f32[64,256]{1,0:T(8,128)S(1)}, f32[64,256]{1,0:T(8,128)S(1)}, u32[]{:S(2)}, u32[]{:S(2)}) %collective-permute-start.6) | collective-permute-done | bytes 65568 | tf_op jit(solution)/shard_map/ppermute | solution.py:405
  36.8 0.3 shard_map.74
  37.1 3.6 %collective-permute-start.9 = (f32[72,256]{1,0:T(8,128)S(1)}, f32[72,256]{1,0:T(8,128)S(1)}, u32[]{:S(2)}, u32[]{:S(2)}) collective-permute-start(f32[72,256]{1,0:T(8,128)S(1)} %get-tuple-element.53), channel_id=1, source_target_pairs={{0,8},{1,9},{2,10},{3,11},{4,12},{5,13},{6,14},{7,15},{8,0},{9,1},... | collective-permute-start | bytes 221192 | tf_op jit(solution)/shard_map/ppermute | solution.py:405
  40.7 2.3 %collective-permute-done.9 = f32[72,256]{1,0:T(8,128)S(1)} collective-permute-done((f32[72,256]{1,0:T(8,128)S(1)}, f32[72,256]{1,0:T(8,128)S(1)}, u32[]{:S(2)}, u32[]{:S(2)}) %collective-permute-start.9) | collective-permute-done | bytes 73760 | tf_op jit(solution)/shard_map/ppermute | solution.py:405
  43.1 0.1 maximum_select_fusion.1
  43.2 0.1 collective-permute-start.10
  43.2 4.3 %collective-permute-done.10 = f32[72,256]{1,0:T(8,128)S(1)} collective-permute-done((f32[72,256]{1,0:T(8,128)S(1)}, f32[72,256]{1,0:T(8,128)S(1)}, u32[]{:S(2)}, u32[]{:S(2)}) %collective-permute-start.10) | collective-permute-done | bytes 73760 | tf_op jit(solution)/shard_map/ppermute | solution.py:405
  47.6 0.1 maximum_select_fusion
  47.7 2.3 %collective-permute-start.11 = (f32[72,256]{1,0:T(8,128)S(1)}, f32[72,256]{1,0:T(8,128)S(1)}, u32[]{:S(2)}, u32[]{:S(2)}) collective-permute-start(f32[72,256]{1,0:T(8,128)S(1)} %maximum_select_fusion), channel_id=1, source_target_pairs={{0,4},{1,5},{2,6},{3,7},{4,0},{5,1},{6,2},{7,3},{8,12},{9,13},{10,... | collective-permute-start | bytes 221192 | tf_op jit(solution)/shard_map/ppermute | solution.py:405
  49.9 2.3 %collective-permute-done.11 = f32[72,256]{1,0:T(8,128)S(1)} collective-permute-done((f32[72,256]{1,0:T(8,128)S(1)}, f32[72,256]{1,0:T(8,128)S(1)}, u32[]{:S(2)}, u32[]{:S(2)}) %collective-permute-start.11) | collective-permute-done | bytes 73760 | tf_op jit(solution)/shard_map/ppermute | solution.py:405
  52.3 0.1 collective-permute-start.12
  52.4 5.0 %collective-permute-done.12 = f32[136,256]{1,0:T(8,128)S(1)} collective-permute-done((f32[136,256]{1,0:T(8,128)S(1)}, f32[136,256]{1,0:T(8,128)S(1)}, u32[]{:S(2)}, u32[]{:S(2)}) %collective-permute-start.12) | collective-permute-done | bytes 139296 | tf_op jit(solution)/shard_map/ppermute | solution.py:405
  57.5 0.1 collective-permute-start.13
  57.6 1.5 %collective-permute-done.13.other = f32[264,256]{1,0:T(8,128)S(1)} collective-permute-done((f32[264,256]{1,0:T(8,128)S(1)}, f32[264,256]{1,0:T(8,128)S(1)}, u32[]{:S(2)}, u32[]{:S(2)}) %collective-permute-start.13) | collective-permute-done | bytes 270368 | tf_op jit(solution)/shard_map/ppermute | solution.py:405
  59.2 1.3 %shard_map.75 = (f32[4,256,256]{2,1,0:T(8,128)}, f32[2,256,256]{2,1,0:T(8,128)}) custom-call(f32[4,256,256]{2,1,0:T(8,128)S(1)} %get-tuple-element.29.obj, f32[4,256,256]{2,1,0:T(8,128)S(1)} %get-tuple-element.50.descent, f32[2,256,256]{2,1,0:T(8,128)S(1)} %get-tuple-element.34.rest_2_.probe, f32[264,256]{1,0:T(8,128)S(1)} %pad_maximum_fusion.mine, ...), custom_call_target="tpu_custom_call" | custom-call | tf_op jit(solution)/shard_map/pallas_call | solution.py:392
  (11 shorter events, 0.2 us)
Async XLA Ops:
  2.1 6.5 %collective-permute-start = (f32[256,128]{1,0:T(8,128)S(1)}, f32[256,128]{1,0:T(8,128)S(1)}, u32[]{:S(2)}, u32[]{:S(2)}) collective-permute-start(f32[256,128]{1,0:T(8,128)S(1)} %get-tuple-element.31), channel_id=1, source_target_pairs={{0,1},{1,0},{2,3},{3,2},{4,5},{5,4},{6,7},{7,6},{8,9},{9,8},{10,11... | collective-permute-start | bytes 393224 | tf_op jit(solution)/shard_map/ppermute | solution.py:413
  5.1 3.5 %collective-permute-start.1 = (f32[256,128]{1,0:T(8,128)S(1)}, f32[256,128]{1,0:T(8,128)S(1)}, u32[]{:S(2)}, u32[]{:S(2)}) collective-permute-start(f32[256,128]{1,0:T(8,128)S(1)} %get-tuple-element.32), channel_id=1, source_target_pairs={{1,2},{2,1},{3,4},{4,3},{5,6},{6,5},{7,8},{8,7},{9,10},{10,9},{11,... | collective-permute-start | bytes 393224 | tf_op jit(solution)/shard_map/ppermute | solution.py:413
  5.8 4.4 %collective-permute-start.2 = (f32[128,256]{1,0:T(8,128)S(1)}, f32[128,256]{1,0:T(8,128)S(1)}, u32[]{:S(2)}, u32[]{:S(2)}) collective-permute-start(f32[128,256]{1,0:T(8,128)S(1)} %get-tuple-element.33), channel_id=1, source_target_pairs={{0,16},{16,0},{1,17},{17,1},{2,18},{18,2},{3,19},{19,3},{4,20},{20... | collective-permute-start | bytes 393224 | tf_op jit(solution)/shard_map/ppermute | solution.py:413
  8.6 1.6 %collective-permute-start.3 = (f32[64,128]{1,0:T(8,128)S(1)}, f32[64,128]{1,0:T(8,128)S(1)}, u32[]{:S(2)}, u32[]{:S(2)}) collective-permute-start(f32[64,128]{1,0:T(8,128)S(1)} %shard_map.70), channel_id=1, source_target_pairs={{0,16},{16,0},{1,17},{17,1},{2,18},{18,2},{3,19},{19,3},{4,20},{20... | collective-permute-start | bytes 98312 | tf_op jit(solution)/shard_map/ppermute | solution.py:413
  19.1 2.0 %collective-permute-start.4 = (f32[416,256]{1,0:T(8,128)S(1)}, f32[416,256]{1,0:T(8,128)S(1)}, u32[]{:S(2)}, u32[]{:S(2)}) collective-permute-start(f32[416,256]{1,0:T(8,128)S(1)} %get-tuple-element.43), channel_id=1, source_target_pairs={{0,16},{16,0},{1,17},{17,1},{2,18},{18,2},{3,19},{19,3},{4,20},{20... | collective-permute-start | bytes 1277960 | tf_op jit(solution)/shard_map/ppermute | solution.py:413
  21.1 9.9 %collective-permute-start.5 = (f32[128,256]{1,0:T(8,128)S(1)}, f32[128,256]{1,0:T(8,128)S(1)}, u32[]{:S(2)}, u32[]{:S(2)}) collective-permute-start(f32[128,256]{1,0:T(8,128)S(1)} %get-tuple-element.45), channel_id=1, source_target_pairs={{0,2},{1,3},{2,0},{3,1},{4,6},{5,7},{6,4},{7,5},{8,10},{9,11},{10,... | collective-permute-start | bytes 393224 | tf_op jit(solution)/shard_map/ppermute | solution.py:405
  27.0 6.8 %collective-permute-start.7 = (f32[128,256]{1,0:T(8,128)S(1)}, f32[128,256]{1,0:T(8,128)S(1)}, u32[]{:S(2)}, u32[]{:S(2)}) collective-permute-start(f32[128,256]{1,0:T(8,128)S(1)} %get-tuple-element.48), channel_id=1, source_target_pairs={{0,1},{1,0},{2,3},{3,2},{4,5},{5,4},{6,7},{7,6},{8,9},{9,8},{10,11... | collective-permute-start | bytes 393224 | tf_op jit(solution)/shard_map/ppermute | solution.py:413
  28.4 5.3 %collective-permute-start.8 = (f32[128,256]{1,0:T(8,128)S(1)}, f32[128,256]{1,0:T(8,128)S(1)}, u32[]{:S(2)}, u32[]{:S(2)}) collective-permute-start(f32[128,256]{1,0:T(8,128)S(1)} %get-tuple-element.49), channel_id=1, source_target_pairs={{1,2},{2,1},{3,4},{4,3},{5,6},{6,5},{7,8},{8,7},{9,10},{10,9},{11,... | collective-permute-start | bytes 393224 | tf_op jit(solution)/shard_map/ppermute | solution.py:413
  31.1 5.7 %collective-permute-start.6 = (f32[64,256]{1,0:T(8,128)S(1)}, f32[64,256]{1,0:T(8,128)S(1)}, u32[]{:S(2)}, u32[]{:S(2)}) collective-permute-start(f32[64,256]{1,0:T(8,128)S(1)} %get-tuple-element.47), channel_id=1, source_target_pairs={{0,4},{1,5},{2,6},{3,7},{4,0},{5,1},{6,2},{7,3},{8,12},{9,13},{10,... | collective-permute-start | bytes 196616 | tf_op jit(solution)/shard_map/ppermute | solution.py:405
  37.1 5.9 %collective-permute-start.9 = (f32[72,256]{1,0:T(8,128)S(1)}, f32[72,256]{1,0:T(8,128)S(1)}, u32[]{:S(2)}, u32[]{:S(2)}) collective-permute-start(f32[72,256]{1,0:T(8,128)S(1)} %get-tuple-element.53), channel_id=1, source_target_pairs={{0,8},{1,9},{2,10},{3,11},{4,12},{5,13},{6,14},{7,15},{8,0},{9,1},... | collective-permute-start | bytes 221192 | tf_op jit(solution)/shard_map/ppermute | solution.py:405
  43.2 4.4 %collective-permute-start.10 = (f32[72,256]{1,0:T(8,128)S(1)}, f32[72,256]{1,0:T(8,128)S(1)}, u32[]{:S(2)}, u32[]{:S(2)}) collective-permute-start(f32[72,256]{1,0:T(8,128)S(1)} %maximum_select_fusion.1), channel_id=1, source_target_pairs={{0,1},{1,0},{2,3},{3,2},{4,5},{5,4},{6,7},{7,6},{8,9},{9,8},{10,11... | collective-permute-start | bytes 221192 | tf_op jit(solution)/shard_map/ppermute | solution.py:405
  47.7 4.6 %collective-permute-start.11 = (f32[72,256]{1,0:T(8,128)S(1)}, f32[72,256]{1,0:T(8,128)S(1)}, u32[]{:S(2)}, u32[]{:S(2)}) collective-permute-start(f32[72,256]{1,0:T(8,128)S(1)} %maximum_select_fusion), channel_id=1, source_target_pairs={{0,4},{1,5},{2,6},{3,7},{4,0},{5,1},{6,2},{7,3},{8,12},{9,13},{10,... | collective-permute-start | bytes 221192 | tf_op jit(solution)/shard_map/ppermute | solution.py:405
  52.3 5.1 %collective-permute-start.12 = (f32[136,256]{1,0:T(8,128)S(1)}, f32[136,256]{1,0:T(8,128)S(1)}, u32[]{:S(2)}, u32[]{:S(2)}) collective-permute-start(f32[136,256]{1,0:T(8,128)S(1)} %pad_maximum_fusion.1), channel_id=1, source_target_pairs={{0,2},{1,3},{2,0},{3,1},{4,6},{5,7},{6,4},{7,5},{8,10},{9,11},{10,... | collective-permute-start | bytes 417800 | tf_op jit(solution)/shard_map/ppermute | solution.py:405
  57.5 1.6 %collective-permute-start.13 = (f32[264,256]{1,0:T(8,128)S(1)}, f32[264,256]{1,0:T(8,128)S(1)}, u32[]{:S(2)}, u32[]{:S(2)}) collective-permute-start(f32[264,256]{1,0:T(8,128)S(1)} %pad_maximum_fusion.mine), channel_id=1, source_target_pairs={{0,16},{16,0},{1,17},{17,1},{2,18},{18,2},{3,19},{19,3},{4,20},{20... | collective-permute-start | bytes 811016 | tf_op jit(solution)/shard_map/ppermute | solution.py:405
